TPU v7x, 32 devices: a whole 2x2x4 slice. The times are simulated.
32 devices in a mesh: dp: 2 (over x), tp: 4 (over z), pp: 4 (over y, core).
Axes of the slice: x: 2, y: 2, z: 4, core: 2. Of those that a mesh axis runs over, the one named last changes fastest.
Arguments:
- x_micro: bfloat16 [16, 64, 1536], P('dp'), parts along dimension 0
- targets: bfloat16 [16, 64, 1536], P('dp'), parts along dimension 0
- w_in: bfloat16 [4, 2, 1536, 6144], P('pp', None, None, 'tp')
- w_out: bfloat16 [4, 2, 6144, 1536], P('pp', None, 'tp')
Outputs:
- output 1: float32 [8, 2, 1536, 6144], P(('dp', 'pp'), None, None, 'tp'), parts along dimension 0
- output 2: float32 [8, 2, 6144, 1536], P(('dp', 'pp'), None, 'tp'), parts along dimension 0
- output 3: float32 [2], P('dp'), parts along dimension 0
There are 2 independent parts. A program takes and returns all parts, laid end to end along the dimension named above; an argument that names none is the same for every part.
All inputs are finite; a program needn't handle non-finite values.
Results may differ from a plain program's by a relative error of at most 0.00675837.
Values are sent between devices in bfloat16 or wider.
A program may use at most 1 GiB of HBM per device.

v0:
```python
import jax
import jax.numpy as jnp
from jax import lax
from jax.sharding import PartitionSpec as P


def gelu_fn(val):
    return jax.nn.gelu(val, approximate=True)


def layer_forward(h_in, w_first, w_second):
    pre_act = jnp.dot(h_in, w_first, preferred_element_type=jnp.float32).astype(jnp.bfloat16)
    hidden = gelu_fn(pre_act.astype(jnp.float32)).astype(jnp.bfloat16)
    partial_sum = jnp.dot(hidden, w_second, preferred_element_type=jnp.float32)
    branch = lax.psum(partial_sum, 'tp')
    return (h_in.astype(jnp.float32) + branch).astype(jnp.bfloat16), pre_act


def layer_backward(grad_h, h_in, pre_act, w_first, w_second):
    grad_hidden = jnp.einsum('bd,fd->bf', grad_h, w_second, preferred_element_type=jnp.float32)
    hidden_f, pull_back = jax.vjp(gelu_fn, pre_act.astype(jnp.float32))
    grad_pre = pull_back(grad_hidden)[0].astype(jnp.bfloat16)
    partial_sum = jnp.einsum('bf,df->bd', grad_pre, w_first, preferred_element_type=jnp.float32)
    grad_in = (grad_h.astype(jnp.float32) + lax.psum(partial_sum, 'tp')).astype(jnp.bfloat16)
    grad_second = jnp.einsum('bf,bd->fd', hidden_f.astype(jnp.bfloat16), grad_h, preferred_element_type=jnp.float32)
    grad_first = jnp.einsum('bd,bf->df', h_in, grad_pre, preferred_element_type=jnp.float32)
    return grad_in, grad_first, grad_second


def solution(mesh):
    n_stage = mesh.shape['pp']
    last = n_stage - 1
    send_down = [(idx, idx + 1) for idx in range(n_stage - 1)]
    send_up = [(idx + 1, idx) for idx in range(n_stage - 1)]

    def stage_body(x_micro, targets, w_in, w_out):
        n_micro, n_token, width = x_micro.shape
        hid_local = w_in.shape[3]
        stage = lax.axis_index('pp')
        norm_factor = 1.0 / (n_micro * n_token * width)
        n_ticks = n_micro + n_stage - 1
        w_first = w_in[0]
        w_second = w_out[0]

        def fwd_tick(tick, carry):
            received, saved_h, saved_pre, saved_grad, loss_sum = carry
            micro_idx = tick - stage
            valid = (micro_idx >= 0) & (micro_idx < n_micro)
            slot = jnp.where(valid, micro_idx, n_micro)
            src_index = jnp.clip(micro_idx, 0, n_micro - 1)
            fresh = lax.dynamic_index_in_dim(x_micro, src_index, 0, keepdims=False)
            h_first = jnp.where(stage == 0, fresh, received)
            h_mid, pre_first = layer_forward(h_first, w_first[0], w_second[0])
            h_out, pre_second = layer_forward(h_mid, w_first[1], w_second[1])
            saved_h = lax.dynamic_update_index_in_dim(saved_h, jnp.stack([h_first, h_mid]), slot, 0)
            saved_pre = lax.dynamic_update_index_in_dim(saved_pre, jnp.stack([pre_first, pre_second]), slot, 0)
            target = lax.dynamic_index_in_dim(targets, src_index, 0, keepdims=False)
            mismatch = h_out.astype(jnp.float32) - target.astype(jnp.float32)
            is_out = valid & (stage == last)
            loss_sum = loss_sum + jnp.where(is_out, 0.5 * jnp.sum(mismatch * mismatch), 0.0)
            saved_grad = lax.dynamic_update_index_in_dim(saved_grad, (mismatch * norm_factor).astype(jnp.bfloat16), slot, 0)
            received = lax.ppermute(h_out, 'pp', send_down)
            return received, saved_h, saved_pre, saved_grad, loss_sum

        fwd_init = (jnp.zeros((n_token, width), jnp.bfloat16), jnp.zeros((n_micro + 1, 2, n_token, width), jnp.bfloat16), jnp.zeros((n_micro + 1, 2, n_token, hid_local), jnp.bfloat16), jnp.zeros((n_micro + 1, n_token, width), jnp.bfloat16), jnp.zeros((), jnp.float32))
        _, saved_h, saved_pre, saved_grad, loss_sum = lax.fori_loop(0, n_ticks, fwd_tick, fwd_init)

        def bwd_tick(tick, carry):
            received, acc_first, acc_second = carry
            micro_idx = tick - (last - stage)
            valid = (micro_idx >= 0) & (micro_idx < n_micro)
            slot = jnp.where(valid, micro_idx, n_micro)
            grad_last = lax.dynamic_index_in_dim(saved_grad, slot, 0, keepdims=False)
            grad_out = jnp.where(stage == last, grad_last, received)
            grad_out = jnp.where(valid, grad_out, jnp.zeros_like(grad_out))
            h_pair = lax.dynamic_index_in_dim(saved_h, slot, 0, keepdims=False)
            pre_pair = lax.dynamic_index_in_dim(saved_pre, slot, 0, keepdims=False)
            grad_mid, first_upper, second_upper = layer_backward(grad_out, h_pair[1], pre_pair[1], w_first[1], w_second[1])
            grad_in, first_lower, second_lower = layer_backward(grad_mid, h_pair[0], pre_pair[0], w_first[0], w_second[0])
            acc_first = acc_first + jnp.stack([first_lower, first_upper])
            acc_second = acc_second + jnp.stack([second_lower, second_upper])
            received = lax.ppermute(grad_in, 'pp', send_up)
            return received, acc_first, acc_second

        bwd_init = (jnp.zeros((n_token, width), jnp.bfloat16), jnp.zeros((2, width, hid_local), jnp.float32), jnp.zeros((2, hid_local, width), jnp.float32))
        _, acc_first, acc_second = lax.fori_loop(0, n_ticks, bwd_tick, bwd_init)
        loss_total = lax.psum(loss_sum, 'pp') * norm_factor
        return acc_first[None], acc_second[None], loss_total.reshape(1)

    data_spec = P('dp', None, None)
    return jax.shard_map(stage_body, mesh=mesh, in_specs=(data_spec, data_spec, P('pp', None, None, 'tp'), P('pp', None, 'tp', None)), out_specs=(P(('dp', 'pp'), None, None, 'tp'), P(('dp', 'pp'), None, 'tp', None), P('dp')), check_vma=False)
```

profile of v0, /device:TPU:0, one launch (start us, length us, event | category | flops | bytes accessed | tf_op | source)
XLA Modules:
  0.0 2587.7 jit_solution(13970911561640316314)
XLA Ops:
  11.6 1093.0 %while.43 = (s32[]{:T(128)}, bf16[64,1536]{1,0:T(8,128)(2,1)S(1)}, bf16[9,2,64,1536]{3,2,1,0:T(8,128)(2,1)}, bf16[9,2,64,1536]{3,2,1,0:T(8,128)(2,1)}, bf16[9,64...) while((s32[]{:T(128)}, bf16[64,1536]{1,0:T(8,128)(2,1)S(1)}, ...), condition=%wide.region_4.5_spmd, body=%wide.region_0.4_spmd.sunk | while | flops 1213562880 | bytes 30867920 | solution.py:66
  19.9 39.9 %all-reduce.5.cloned.1.call-done = f32[64,1536]{1,0:T(8,128)} async-done(((f32[64,1536]{1,0:T(8,128)}), f32[64,1536]{1,0:T(8,128)}) %all-reduce.5.cloned.1.call-update) | async-done | bytes 393232 | tf_op jit(solution)/shard_map/while/body/eval_jaxpr/psum | solution.py:15
  69.1 36.0 %all-reduce.7.cloned.1.call-done = f32[64,1536]{1,0:T(8,128)} async-done(((f32[64,1536]{1,0:T(8,128)}), f32[64,1536]{1,0:T(8,128)}) %all-reduce.7.cloned.1.call-update) | async-done | bytes 393232 | tf_op jit(solution)/shard_map/while/body/eval_jaxpr/psum | solution.py:15
  118.3 41.0 %all-reduce.5.cloned.1.call-done = f32[64,1536]{1,0:T(8,128)} async-done(((f32[64,1536]{1,0:T(8,128)}), f32[64,1536]{1,0:T(8,128)}) %all-reduce.5.cloned.1.call-update) | async-done | bytes 393232 | tf_op jit(solution)/shard_map/while/body/eval_jaxpr/psum | solution.py:15
  168.6 36.1 %all-reduce.7.cloned.1.call-done = f32[64,1536]{1,0:T(8,128)} async-done(((f32[64,1536]{1,0:T(8,128)}), f32[64,1536]{1,0:T(8,128)}) %all-reduce.7.cloned.1.call-update) | async-done | bytes 393232 | tf_op jit(solution)/shard_map/while/body/eval_jaxpr/psum | solution.py:15
  217.8 40.9 %all-reduce.5.cloned.1.call-done = f32[64,1536]{1,0:T(8,128)} async-done(((f32[64,1536]{1,0:T(8,128)}), f32[64,1536]{1,0:T(8,128)}) %all-reduce.5.cloned.1.call-update) | async-done | bytes 393232 | tf_op jit(solution)/shard_map/while/body/eval_jaxpr/psum | solution.py:15
  268.0 36.1 %all-reduce.7.cloned.1.call-done = f32[64,1536]{1,0:T(8,128)} async-done(((f32[64,1536]{1,0:T(8,128)}), f32[64,1536]{1,0:T(8,128)}) %all-reduce.7.cloned.1.call-update) | async-done | bytes 393232 | tf_op jit(solution)/shard_map/while/body/eval_jaxpr/psum | solution.py:15
  317.3 40.9 %all-reduce.5.cloned.1.call-done = f32[64,1536]{1,0:T(8,128)} async-done(((f32[64,1536]{1,0:T(8,128)}), f32[64,1536]{1,0:T(8,128)}) %all-reduce.5.cloned.1.call-update) | async-done | bytes 393232 | tf_op jit(solution)/shard_map/while/body/eval_jaxpr/psum | solution.py:15
  367.5 36.1 %all-reduce.7.cloned.1.call-done = f32[64,1536]{1,0:T(8,128)} async-done(((f32[64,1536]{1,0:T(8,128)}), f32[64,1536]{1,0:T(8,128)}) %all-reduce.7.cloned.1.call-update) | async-done | bytes 393232 | tf_op jit(solution)/shard_map/while/body/eval_jaxpr/psum | solution.py:15
  416.7 41.0 %all-reduce.5.cloned.1.call-done = f32[64,1536]{1,0:T(8,128)} async-done(((f32[64,1536]{1,0:T(8,128)}), f32[64,1536]{1,0:T(8,128)}) %all-reduce.5.cloned.1.call-update) | async-done | bytes 393232 | tf_op jit(solution)/shard_map/while/body/eval_jaxpr/psum | solution.py:15
  467.0 36.1 %all-reduce.7.cloned.1.call-done = f32[64,1536]{1,0:T(8,128)} async-done(((f32[64,1536]{1,0:T(8,128)}), f32[64,1536]{1,0:T(8,128)}) %all-reduce.7.cloned.1.call-update) | async-done | bytes 393232 | tf_op jit(solution)/shard_map/while/body/eval_jaxpr/psum | solution.py:15
  516.2 40.9 %all-reduce.5.cloned.1.call-done = f32[64,1536]{1,0:T(8,128)} async-done(((f32[64,1536]{1,0:T(8,128)}), f32[64,1536]{1,0:T(8,128)}) %all-reduce.5.cloned.1.call-update) | async-done | bytes 393232 | tf_op jit(solution)/shard_map/while/body/eval_jaxpr/psum | solution.py:15
  566.5 36.0 %all-reduce.7.cloned.1.call-done = f32[64,1536]{1,0:T(8,128)} async-done(((f32[64,1536]{1,0:T(8,128)}), f32[64,1536]{1,0:T(8,128)}) %all-reduce.7.cloned.1.call-update) | async-done | bytes 393232 | tf_op jit(solution)/shard_map/while/body/eval_jaxpr/psum | solution.py:15
  615.7 40.9 %all-reduce.5.cloned.1.call-done = f32[64,1536]{1,0:T(8,128)} async-done(((f32[64,1536]{1,0:T(8,128)}), f32[64,1536]{1,0:T(8,128)}) %all-reduce.5.cloned.1.call-update) | async-done | bytes 393232 | tf_op jit(solution)/shard_map/while/body/eval_jaxpr/psum | solution.py:15
  665.9 36.1 %all-reduce.7.cloned.1.call-done = f32[64,1536]{1,0:T(8,128)} async-done(((f32[64,1536]{1,0:T(8,128)}), f32[64,1536]{1,0:T(8,128)}) %all-reduce.7.cloned.1.call-update) | async-done | bytes 393232 | tf_op jit(solution)/shard_map/while/body/eval_jaxpr/psum | solution.py:15
  715.1 41.0 %all-reduce.5.cloned.1.call-done = f32[64,1536]{1,0:T(8,128)} async-done(((f32[64,1536]{1,0:T(8,128)}), f32[64,1536]{1,0:T(8,128)}) %all-reduce.5.cloned.1.call-update) | async-done | bytes 393232 | tf_op jit(solution)/shard_map/while/body/eval_jaxpr/psum | solution.py:15
  765.4 36.0 %all-reduce.7.cloned.1.call-done = f32[64,1536]{1,0:T(8,128)} async-done(((f32[64,1536]{1,0:T(8,128)}), f32[64,1536]{1,0:T(8,128)}) %all-reduce.7.cloned.1.call-update) | async-done | bytes 393232 | tf_op jit(solution)/shard_map/while/body/eval_jaxpr/psum | solution.py:15
  814.6 40.9 %all-reduce.5.cloned.1.call-done = f32[64,1536]{1,0:T(8,128)} async-done(((f32[64,1536]{1,0:T(8,128)}), f32[64,1536]{1,0:T(8,128)}) %all-reduce.5.cloned.1.call-update) | async-done | bytes 393232 | tf_op jit(solution)/shard_map/while/body/eval_jaxpr/psum | solution.py:15
  864.9 36.0 %all-reduce.7.cloned.1.call-done = f32[64,1536]{1,0:T(8,128)} async-done(((f32[64,1536]{1,0:T(8,128)}), f32[64,1536]{1,0:T(8,128)}) %all-reduce.7.cloned.1.call-update) | async-done | bytes 393232 | tf_op jit(solution)/shard_map/while/body/eval_jaxpr/psum | solution.py:15
  914.1 40.9 %all-reduce.5.cloned.1.call-done = f32[64,1536]{1,0:T(8,128)} async-done(((f32[64,1536]{1,0:T(8,128)}), f32[64,1536]{1,0:T(8,128)}) %all-reduce.5.cloned.1.call-update) | async-done | bytes 393232 | tf_op jit(solution)/shard_map/while/body/eval_jaxpr/psum | solution.py:15
  964.3 36.0 %all-reduce.7.cloned.1.call-done = f32[64,1536]{1,0:T(8,128)} async-done(((f32[64,1536]{1,0:T(8,128)}), f32[64,1536]{1,0:T(8,128)}) %all-reduce.7.cloned.1.call-update) | async-done | bytes 393232 | tf_op jit(solution)/shard_map/while/body/eval_jaxpr/psum | solution.py:15
  1013.5 41.0 %all-reduce.5.cloned.1.call-done = f32[64,1536]{1,0:T(8,128)} async-done(((f32[64,1536]{1,0:T(8,128)}), f32[64,1536]{1,0:T(8,128)}) %all-reduce.5.cloned.1.call-update) | async-done | bytes 393232 | tf_op jit(solution)/shard_map/while/body/eval_jaxpr/psum | solution.py:15
  1063.8 36.0 %all-reduce.7.cloned.1.call-done = f32[64,1536]{1,0:T(8,128)} async-done(((f32[64,1536]{1,0:T(8,128)}), f32[64,1536]{1,0:T(8,128)}) %all-reduce.7.cloned.1.call-update) | async-done | bytes 393232 | tf_op jit(solution)/shard_map/while/body/eval_jaxpr/psum | solution.py:15
  1115.7 1464.3 %while.44 = (s32[]{:T(128)}, bf16[64,1536]{1,0:T(8,128)(2,1)S(1)}, f32[2,1536,1536]{2,1,0:T(8,128)}, f32[2,1536,1536]{2,1,0:T(8,128)}, s32[]{:T(128)}, /*index=5...) while((s32[]{:T(128)}, bf16[64,1536]{1,0:T(8,128)(2,1)S(1)}, ...), condition=%wide.region_8.9_spmd.clone, body=%wide.region_5.8_spmd.clone.sunk | while | flops 2451308544 | bytes 181469600 | solution.py:86
  1130.5 31.7 %all-reduce.9.cloned.1.call-done = f32[64,1536]{1,0:T(8,128)} async-done(((f32[64,1536]{1,0:T(8,128)}), f32[64,1536]{1,0:T(8,128)}) %all-reduce.9.cloned.1.call-update) | async-done | bytes 393232 | tf_op jit(solution)/shard_map/while/body/eval_jaxpr/psum | solution.py:24
  1189.8 19.0 all-reduce.11.cloned.1.call-done
  1211.1 29.1 %maximum_add_fusion.3 = (f32[2,1536,1536]{2,1,0:T(8,128)}, f32[2,1536,1536]{2,1,0:T(8,128)}) fusion(f32[1,1536,1536]{2,1,0:T(8,128)} %convolution_bitcast_fusion.8, f32[1,1536,1536]{2,1,0:T(8,128)} %convolution_bitcast_fusion.9, f32[2,1536,1536]{2,1,0:T(8,128)} %get-tuple-element.854, pred[]{:T(512)S(6)} %compare.3, ...), kind=kLoop, calls=%fused_computation.62.clone.1 | loop fusion | flops 28311552 | bytes 113246208 | tf_op jit(solution)/shard_map/while/body/eval_jaxpr/add | solution.py:80
  1254.9 31.8 %all-reduce.9.cloned.1.call-done = f32[64,1536]{1,0:T(8,128)} async-done(((f32[64,1536]{1,0:T(8,128)}), f32[64,1536]{1,0:T(8,128)}) %all-reduce.9.cloned.1.call-update) | async-done | bytes 393232 | tf_op jit(solution)/shard_map/while/body/eval_jaxpr/psum | solution.py:24
  1314.4 19.0 all-reduce.11.cloned.1.call-done
  1335.7 38.5 %maximum_add_fusion.3 = (f32[2,1536,1536]{2,1,0:T(8,128)}, f32[2,1536,1536]{2,1,0:T(8,128)}) fusion(f32[1,1536,1536]{2,1,0:T(8,128)} %convolution_bitcast_fusion.8, f32[1,1536,1536]{2,1,0:T(8,128)} %convolution_bitcast_fusion.9, f32[2,1536,1536]{2,1,0:T(8,128)} %get-tuple-element.854, pred[]{:T(512)S(6)} %compare.3, ...), kind=kLoop, calls=%fused_computation.62.clone.1 | loop fusion | flops 28311552 | bytes 113246208 | tf_op jit(solution)/shard_map/while/body/eval_jaxpr/add | solution.py:80
  1389.0 31.8 %all-reduce.9.cloned.1.call-done = f32[64,1536]{1,0:T(8,128)} async-done(((f32[64,1536]{1,0:T(8,128)}), f32[64,1536]{1,0:T(8,128)}) %all-reduce.9.cloned.1.call-update) | async-done | bytes 393232 | tf_op jit(solution)/shard_map/while/body/eval_jaxpr/psum | solution.py:24
  1469.7 38.5 %maximum_add_fusion.3 = (f32[2,1536,1536]{2,1,0:T(8,128)}, f32[2,1536,1536]{2,1,0:T(8,128)}) fusion(f32[1,1536,1536]{2,1,0:T(8,128)} %convolution_bitcast_fusion.8, f32[1,1536,1536]{2,1,0:T(8,128)} %convolution_bitcast_fusion.9, f32[2,1536,1536]{2,1,0:T(8,128)} %get-tuple-element.854, pred[]{:T(512)S(6)} %compare.3, ...), kind=kLoop, calls=%fused_computation.62.clone.1 | loop fusion | flops 28311552 | bytes 113246208 | tf_op jit(solution)/shard_map/while/body/eval_jaxpr/add | solution.py:80
  1522.9 31.8 %all-reduce.9.cloned.1.call-done = f32[64,1536]{1,0:T(8,128)} async-done(((f32[64,1536]{1,0:T(8,128)}), f32[64,1536]{1,0:T(8,128)}) %all-reduce.9.cloned.1.call-update) | async-done | bytes 393232 | tf_op jit(solution)/shard_map/while/body/eval_jaxpr/psum | solution.py:24
  1603.7 38.5 %maximum_add_fusion.3 = (f32[2,1536,1536]{2,1,0:T(8,128)}, f32[2,1536,1536]{2,1,0:T(8,128)}) fusion(f32[1,1536,1536]{2,1,0:T(8,128)} %convolution_bitcast_fusion.8, f32[1,1536,1536]{2,1,0:T(8,128)} %convolution_bitcast_fusion.9, f32[2,1536,1536]{2,1,0:T(8,128)} %get-tuple-element.854, pred[]{:T(512)S(6)} %compare.3, ...), kind=kLoop, calls=%fused_computation.62.clone.1 | loop fusion | flops 28311552 | bytes 113246208 | tf_op jit(solution)/shard_map/while/body/eval_jaxpr/add | solution.py:80
  1656.9 31.7 %all-reduce.9.cloned.1.call-done = f32[64,1536]{1,0:T(8,128)} async-done(((f32[64,1536]{1,0:T(8,128)}), f32[64,1536]{1,0:T(8,128)}) %all-reduce.9.cloned.1.call-update) | async-done | bytes 393232 | tf_op jit(solution)/shard_map/while/body/eval_jaxpr/psum | solution.py:24
  1737.6 38.5 %maximum_add_fusion.3 = (f32[2,1536,1536]{2,1,0:T(8,128)}, f32[2,1536,1536]{2,1,0:T(8,128)}) fusion(f32[1,1536,1536]{2,1,0:T(8,128)} %convolution_bitcast_fusion.8, f32[1,1536,1536]{2,1,0:T(8,128)} %convolution_bitcast_fusion.9, f32[2,1536,1536]{2,1,0:T(8,128)} %get-tuple-element.854, pred[]{:T(512)S(6)} %compare.3, ...), kind=kLoop, calls=%fused_computation.62.clone.1 | loop fusion | flops 28311552 | bytes 113246208 | tf_op jit(solution)/shard_map/while/body/eval_jaxpr/add | solution.py:80
  1790.9 31.8 %all-reduce.9.cloned.1.call-done = f32[64,1536]{1,0:T(8,128)} async-done(((f32[64,1536]{1,0:T(8,128)}), f32[64,1536]{1,0:T(8,128)}) %all-reduce.9.cloned.1.call-update) | async-done | bytes 393232 | tf_op jit(solution)/shard_map/while/body/eval_jaxpr/psum | solution.py:24
  1871.6 38.5 %maximum_add_fusion.3 = (f32[2,1536,1536]{2,1,0:T(8,128)}, f32[2,1536,1536]{2,1,0:T(8,128)}) fusion(f32[1,1536,1536]{2,1,0:T(8,128)} %convolution_bitcast_fusion.8, f32[1,1536,1536]{2,1,0:T(8,128)} %convolution_bitcast_fusion.9, f32[2,1536,1536]{2,1,0:T(8,128)} %get-tuple-element.854, pred[]{:T(512)S(6)} %compare.3, ...), kind=kLoop, calls=%fused_computation.62.clone.1 | loop fusion | flops 28311552 | bytes 113246208 | tf_op jit(solution)/shard_map/while/body/eval_jaxpr/add | solution.py:80
  1924.8 31.8 %all-reduce.9.cloned.1.call-done = f32[64,1536]{1,0:T(8,128)} async-done(((f32[64,1536]{1,0:T(8,128)}), f32[64,1536]{1,0:T(8,128)}) %all-reduce.9.cloned.1.call-update) | async-done | bytes 393232 | tf_op jit(solution)/shard_map/while/body/eval_jaxpr/psum | solution.py:24
  2005.5 38.5 %maximum_add_fusion.3 = (f32[2,1536,1536]{2,1,0:T(8,128)}, f32[2,1536,1536]{2,1,0:T(8,128)}) fusion(f32[1,1536,1536]{2,1,0:T(8,128)} %convolution_bitcast_fusion.8, f32[1,1536,1536]{2,1,0:T(8,128)} %convolution_bitcast_fusion.9, f32[2,1536,1536]{2,1,0:T(8,128)} %get-tuple-element.854, pred[]{:T(512)S(6)} %compare.3, ...), kind=kLoop, calls=%fused_computation.62.clone.1 | loop fusion | flops 28311552 | bytes 113246208 | tf_op jit(solution)/shard_map/while/body/eval_jaxpr/add | solution.py:80
  2058.8 31.8 %all-reduce.9.cloned.1.call-done = f32[64,1536]{1,0:T(8,128)} async-done(((f32[64,1536]{1,0:T(8,128)}), f32[64,1536]{1,0:T(8,128)}) %all-reduce.9.cloned.1.call-update) | async-done | bytes 393232 | tf_op jit(solution)/shard_map/while/body/eval_jaxpr/psum | solution.py:24
  2139.6 38.5 %maximum_add_fusion.3 = (f32[2,1536,1536]{2,1,0:T(8,128)}, f32[2,1536,1536]{2,1,0:T(8,128)}) fusion(f32[1,1536,1536]{2,1,0:T(8,128)} %convolution_bitcast_fusion.8, f32[1,1536,1536]{2,1,0:T(8,128)} %convolution_bitcast_fusion.9, f32[2,1536,1536]{2,1,0:T(8,128)} %get-tuple-element.854, pred[]{:T(512)S(6)} %compare.3, ...), kind=kLoop, calls=%fused_computation.62.clone.1 | loop fusion | flops 28311552 | bytes 113246208 | tf_op jit(solution)/shard_map/while/body/eval_jaxpr/add | solution.py:80
  2192.8 31.8 %all-reduce.9.cloned.1.call-done = f32[64,1536]{1,0:T(8,128)} async-done(((f32[64,1536]{1,0:T(8,128)}), f32[64,1536]{1,0:T(8,128)}) %all-reduce.9.cloned.1.call-update) | async-done | bytes 393232 | tf_op jit(solution)/shard_map/while/body/eval_jaxpr/psum | solution.py:24
  2273.5 38.5 %maximum_add_fusion.3 = (f32[2,1536,1536]{2,1,0:T(8,128)}, f32[2,1536,1536]{2,1,0:T(8,128)}) fusion(f32[1,1536,1536]{2,1,0:T(8,128)} %convolution_bitcast_fusion.8, f32[1,1536,1536]{2,1,0:T(8,128)} %convolution_bitcast_fusion.9, f32[2,1536,1536]{2,1,0:T(8,128)} %get-tuple-element.854, pred[]{:T(512)S(6)} %compare.3, ...), kind=kLoop, calls=%fused_computation.62.clone.1 | loop fusion | flops 28311552 | bytes 113246208 | tf_op jit(solution)/shard_map/while/body/eval_jaxpr/add | solution.py:80
  2326.8 31.8 %all-reduce.9.cloned.1.call-done = f32[64,1536]{1,0:T(8,128)} async-done(((f32[64,1536]{1,0:T(8,128)}), f32[64,1536]{1,0:T(8,128)}) %all-reduce.9.cloned.1.call-update) | async-done | bytes 393232 | tf_op jit(solution)/shard_map/while/body/eval_jaxpr/psum | solution.py:24
  2407.5 38.5 %maximum_add_fusion.3 = (f32[2,1536,1536]{2,1,0:T(8,128)}, f32[2,1536,1536]{2,1,0:T(8,128)}) fusion(f32[1,1536,1536]{2,1,0:T(8,128)} %convolution_bitcast_fusion.8, f32[1,1536,1536]{2,1,0:T(8,128)} %convolution_bitcast_fusion.9, f32[2,1536,1536]{2,1,0:T(8,128)} %get-tuple-element.854, pred[]{:T(512)S(6)} %compare.3, ...), kind=kLoop, calls=%fused_computation.62.clone.1 | loop fusion | flops 28311552 | bytes 113246208 | tf_op jit(solution)/shard_map/while/body/eval_jaxpr/add | solution.py:80
  2460.8 31.8 %all-reduce.9.cloned.1.call-done = f32[64,1536]{1,0:T(8,128)} async-done(((f32[64,1536]{1,0:T(8,128)}), f32[64,1536]{1,0:T(8,128)}) %all-reduce.9.cloned.1.call-update) | async-done | bytes 393232 | tf_op jit(solution)/shard_map/while/body/eval_jaxpr/psum | solution.py:24
  2541.5 38.5 %maximum_add_fusion.3 = (f32[2,1536,1536]{2,1,0:T(8,128)}, f32[2,1536,1536]{2,1,0:T(8,128)}) fusion(f32[1,1536,1536]{2,1,0:T(8,128)} %convolution_bitcast_fusion.8, f32[1,1536,1536]{2,1,0:T(8,128)} %convolution_bitcast_fusion.9, f32[2,1536,1536]{2,1,0:T(8,128)} %get-tuple-element.854, pred[]{:T(512)S(6)} %compare.3, ...), kind=kLoop, calls=%fused_computation.62.clone.1 | loop fusion | flops 28311552 | bytes 113246208 | tf_op jit(solution)/shard_map/while/body/eval_jaxpr/add | solution.py:80
  (369 shorter events, 915.4 us)
Async XLA Ops:
  11.6 48.2 %all-reduce.5.cloned.1.call-start = ((), (), s32[]{:S(2)}) async-start(), calls=%async_computation | async-start | bytes 786432 | tf_op jit(solution)/shard_map/while/body/eval_jaxpr/psum | solution.py:15
  19.9 85.3 %all-reduce.7.cloned.1.call-start = ((), (), s32[]{:S(2)}) async-start(), calls=%async_computation.1 | async-start | bytes 786432 | tf_op jit(solution)/shard_map/while/body/eval_jaxpr/psum | solution.py:15
  109.9 49.3 %all-reduce.5.cloned.1.call-start = ((), (), s32[]{:S(2)}) async-start(), calls=%async_computation | async-start | bytes 786432 | tf_op jit(solution)/shard_map/while/body/eval_jaxpr/psum | solution.py:15
  118.3 86.4 %all-reduce.7.cloned.1.call-start = ((), (), s32[]{:S(2)}) async-start(), calls=%async_computation.1 | async-start | bytes 786432 | tf_op jit(solution)/shard_map/while/body/eval_jaxpr/psum | solution.py:15
  209.4 49.3 %all-reduce.5.cloned.1.call-start = ((), (), s32[]{:S(2)}) async-start(), calls=%async_computation | async-start | bytes 786432 | tf_op jit(solution)/shard_map/while/body/eval_jaxpr/psum | solution.py:15
  217.7 86.4 %all-reduce.7.cloned.1.call-start = ((), (), s32[]{:S(2)}) async-start(), calls=%async_computation.1 | async-start | bytes 786432 | tf_op jit(solution)/shard_map/while/body/eval_jaxpr/psum | solution.py:15
  308.9 49.3 %all-reduce.5.cloned.1.call-start = ((), (), s32[]{:S(2)}) async-start(), calls=%async_computation | async-start | bytes 786432 | tf_op jit(solution)/shard_map/while/body/eval_jaxpr/psum | solution.py:15
  317.2 86.3 %all-reduce.7.cloned.1.call-start = ((), (), s32[]{:S(2)}) async-start(), calls=%async_computation.1 | async-start | bytes 786432 | tf_op jit(solution)/shard_map/while/body/eval_jaxpr/psum | solution.py:15
  408.3 49.3 %all-reduce.5.cloned.1.call-start = ((), (), s32[]{:S(2)}) async-start(), calls=%async_computation | async-start | bytes 786432 | tf_op jit(solution)/shard_map/while/body/eval_jaxpr/psum | solution.py:15
  416.7 86.4 %all-reduce.7.cloned.1.call-start = ((), (), s32[]{:S(2)}) async-start(), calls=%async_computation.1 | async-start | bytes 786432 | tf_op jit(solution)/shard_map/while/body/eval_jaxpr/psum | solution.py:15
  507.8 49.3 %all-reduce.5.cloned.1.call-start = ((), (), s32[]{:S(2)}) async-start(), calls=%async_computation | async-start | bytes 786432 | tf_op jit(solution)/shard_map/while/body/eval_jaxpr/psum | solution.py:15
  516.1 86.4 %all-reduce.7.cloned.1.call-start = ((), (), s32[]{:S(2)}) async-start(), calls=%async_computation.1 | async-start | bytes 786432 | tf_op jit(solution)/shard_map/while/body/eval_jaxpr/psum | solution.py:15
  607.3 49.3 %all-reduce.5.cloned.1.call-start = ((), (), s32[]{:S(2)}) async-start(), calls=%async_computation | async-start | bytes 786432 | tf_op jit(solution)/shard_map/while/body/eval_jaxpr/psum | solution.py:15
  615.6 86.3 %all-reduce.7.cloned.1.call-start = ((), (), s32[]{:S(2)}) async-start(), calls=%async_computation.1 | async-start | bytes 786432 | tf_op jit(solution)/shard_map/while/body/eval_jaxpr/psum | solution.py:15
  706.7 49.3 %all-reduce.5.cloned.1.call-start = ((), (), s32[]{:S(2)}) async-start(), calls=%async_computation | async-start | bytes 786432 | tf_op jit(solution)/shard_map/while/body/eval_jaxpr/psum | solution.py:15
  715.1 86.4 %all-reduce.7.cloned.1.call-start = ((), (), s32[]{:S(2)}) async-start(), calls=%async_computation.1 | async-start | bytes 786432 | tf_op jit(solution)/shard_map/while/body/eval_jaxpr/psum | solution.py:15
  806.2 49.3 %all-reduce.5.cloned.1.call-start = ((), (), s32[]{:S(2)}) async-start(), calls=%async_computation | async-start | bytes 786432 | tf_op jit(solution)/shard_map/while/body/eval_jaxpr/psum | solution.py:15
  814.5 86.4 %all-reduce.7.cloned.1.call-start = ((), (), s32[]{:S(2)}) async-start(), calls=%async_computation.1 | async-start | bytes 786432 | tf_op jit(solution)/shard_map/while/body/eval_jaxpr/psum | solution.py:15
  905.7 49.3 %all-reduce.5.cloned.1.call-start = ((), (), s32[]{:S(2)}) async-start(), calls=%async_computation | async-start | bytes 786432 | tf_op jit(solution)/shard_map/while/body/eval_jaxpr/psum | solution.py:15
  914.0 86.3 %all-reduce.7.cloned.1.call-start = ((), (), s32[]{:S(2)}) async-start(), calls=%async_computation.1 | async-start | bytes 786432 | tf_op jit(solution)/shard_map/while/body/eval_jaxpr/psum | solution.py:15
  1005.1 49.3 %all-reduce.5.cloned.1.call-start = ((), (), s32[]{:S(2)}) async-start(), calls=%async_computation | async-start | bytes 786432 | tf_op jit(solution)/shard_map/while/body/eval_jaxpr/psum | solution.py:15
  1013.5 86.4 %all-reduce.7.cloned.1.call-start = ((), (), s32[]{:S(2)}) async-start(), calls=%async_computation.1 | async-start | bytes 786432 | tf_op jit(solution)/shard_map/while/body/eval_jaxpr/psum | solution.py:15
  1115.7 46.4 %all-reduce.9.cloned.1.call-start = ((), (), s32[]{:S(2)}) async-start(), calls=%async_computation.2 | async-start | bytes 786432 | tf_op jit(solution)/shard_map/while/body/eval_jaxpr/psum | solution.py:24
  1124.4 84.4 %all-reduce.11.cloned.1.call-start = ((), (), s32[]{:S(2)}) async-start(), calls=%async_computation.3 | async-start | bytes 786432 | tf_op jit(solution)/shard_map/while/body/eval_jaxpr/psum | solution.py:24
  1240.2 46.5 %all-reduce.9.cloned.1.call-start = ((), (), s32[]{:S(2)}) async-start(), calls=%async_computation.2 | async-start | bytes 786432 | tf_op jit(solution)/shard_map/while/body/eval_jaxpr/psum | solution.py:24
  1248.9 84.5 %all-reduce.11.cloned.1.call-start = ((), (), s32[]{:S(2)}) async-start(), calls=%async_computation.3 | async-start | bytes 786432 | tf_op jit(solution)/shard_map/while/body/eval_jaxpr/psum | solution.py:24
  1334.4 39.8 %collective-permute-start.1 = (bf16[64,1536]{1,0:T(8,128)(2,1)S(1)}, bf16[64,1536]{1,0:T(8,128)(2,1)S(1)}, u32[]{:S(2)}, u32[]{:S(2)}) collective-permute-start(bf16[64,1536]{1,0:T(8,128)(2,1)S(1)} %add_convert_fusion.10), channel_id=1, source_target_pairs={{1,0},{2,1},{3,2},{5,4},{6,5},{7,6},{9,8},{10,9},{11,10},{13,12},{... | collective-permute-start | bytes 589832 | tf_op jit(solution)/shard_map/while/body/eval_jaxpr/ppermute | solution.py:82
  1374.2 46.5 %all-reduce.9.cloned.1.call-start = ((), (), s32[]{:S(2)}) async-start(), calls=%async_computation.2 | async-start | bytes 786432 | tf_op jit(solution)/shard_map/while/body/eval_jaxpr/psum | solution.py:24
  1382.9 84.4 %all-reduce.11.cloned.1.call-start = ((), (), s32[]{:S(2)}) async-start(), calls=%async_computation.3 | async-start | bytes 786432 | tf_op jit(solution)/shard_map/while/body/eval_jaxpr/psum | solution.py:24
  1468.4 39.8 %collective-permute-start.1 = (bf16[64,1536]{1,0:T(8,128)(2,1)S(1)}, bf16[64,1536]{1,0:T(8,128)(2,1)S(1)}, u32[]{:S(2)}, u32[]{:S(2)}) collective-permute-start(bf16[64,1536]{1,0:T(8,128)(2,1)S(1)} %add_convert_fusion.10), channel_id=1, source_target_pairs={{1,0},{2,1},{3,2},{5,4},{6,5},{7,6},{9,8},{10,9},{11,10},{13,12},{... | collective-permute-start | bytes 589832 | tf_op jit(solution)/shard_map/while/body/eval_jaxpr/ppermute | solution.py:82
  1508.2 46.5 %all-reduce.9.cloned.1.call-start = ((), (), s32[]{:S(2)}) async-start(), calls=%async_computation.2 | async-start | bytes 786432 | tf_op jit(solution)/shard_map/while/body/eval_jaxpr/psum | solution.py:24
  1516.9 84.4 %all-reduce.11.cloned.1.call-start = ((), (), s32[]{:S(2)}) async-start(), calls=%async_computation.3 | async-start | bytes 786432 | tf_op jit(solution)/shard_map/while/body/eval_jaxpr/psum | solution.py:24
  1602.4 39.8 %collective-permute-start.1 = (bf16[64,1536]{1,0:T(8,128)(2,1)S(1)}, bf16[64,1536]{1,0:T(8,128)(2,1)S(1)}, u32[]{:S(2)}, u32[]{:S(2)}) collective-permute-start(bf16[64,1536]{1,0:T(8,128)(2,1)S(1)} %add_convert_fusion.10), channel_id=1, source_target_pairs={{1,0},{2,1},{3,2},{5,4},{6,5},{7,6},{9,8},{10,9},{11,10},{13,12},{... | collective-permute-start | bytes 589832 | tf_op jit(solution)/shard_map/while/body/eval_jaxpr/ppermute | solution.py:82
  1642.2 46.5 %all-reduce.9.cloned.1.call-start = ((), (), s32[]{:S(2)}) async-start(), calls=%async_computation.2 | async-start | bytes 786432 | tf_op jit(solution)/shard_map/while/body/eval_jaxpr/psum | solution.py:24
  1650.9 84.4 %all-reduce.11.cloned.1.call-start = ((), (), s32[]{:S(2)}) async-start(), calls=%async_computation.3 | async-start | bytes 786432 | tf_op jit(solution)/shard_map/while/body/eval_jaxpr/psum | solution.py:24
  1736.3 39.8 %collective-permute-start.1 = (bf16[64,1536]{1,0:T(8,128)(2,1)S(1)}, bf16[64,1536]{1,0:T(8,128)(2,1)S(1)}, u32[]{:S(2)}, u32[]{:S(2)}) collective-permute-start(bf16[64,1536]{1,0:T(8,128)(2,1)S(1)} %add_convert_fusion.10), channel_id=1, source_target_pairs={{1,0},{2,1},{3,2},{5,4},{6,5},{7,6},{9,8},{10,9},{11,10},{13,12},{... | collective-permute-start | bytes 589832 | tf_op jit(solution)/shard_map/while/body/eval_jaxpr/ppermute | solution.py:82
  1776.1 46.5 %all-reduce.9.cloned.1.call-start = ((), (), s32[]{:S(2)}) async-start(), calls=%async_computation.2 | async-start | bytes 786432 | tf_op jit(solution)/shard_map/while/body/eval_jaxpr/psum | solution.py:24
  1784.8 84.4 %all-reduce.11.cloned.1.call-start = ((), (), s32[]{:S(2)}) async-start(), calls=%async_computation.3 | async-start | bytes 786432 | tf_op jit(solution)/shard_map/while/body/eval_jaxpr/psum | solution.py:24
  1910.1 46.5 %all-reduce.9.cloned.1.call-start = ((), (), s32[]{:S(2)}) async-start(), calls=%async_computation.2 | async-start | bytes 786432 | tf_op jit(solution)/shard_map/while/body/eval_jaxpr/psum | solution.py:24
  1918.8 84.4 %all-reduce.11.cloned.1.call-start = ((), (), s32[]{:S(2)}) async-start(), calls=%async_computation.3 | async-start | bytes 786432 | tf_op jit(solution)/shard_map/while/body/eval_jaxpr/psum | solution.py:24
  2044.0 46.5 %all-reduce.9.cloned.1.call-start = ((), (), s32[]{:S(2)}) async-start(), calls=%async_computation.2 | async-start | bytes 786432 | tf_op jit(solution)/shard_map/while/body/eval_jaxpr/psum | solution.py:24
  2052.8 84.5 %all-reduce.11.cloned.1.call-start = ((), (), s32[]{:S(2)}) async-start(), calls=%async_computation.3 | async-start | bytes 786432 | tf_op jit(solution)/shard_map/while/body/eval_jaxpr/psum | solution.py:24
  2178.1 46.5 %all-reduce.9.cloned.1.call-start = ((), (), s32[]{:S(2)}) async-start(), calls=%async_computation.2 | async-start | bytes 786432 | tf_op jit(solution)/shard_map/while/body/eval_jaxpr/psum | solution.py:24
  2186.8 84.4 %all-reduce.11.cloned.1.call-start = ((), (), s32[]{:S(2)}) async-start(), calls=%async_computation.3 | async-start | bytes 786432 | tf_op jit(solution)/shard_map/while/body/eval_jaxpr/psum | solution.py:24
  2312.0 46.5 %all-reduce.9.cloned.1.call-start = ((), (), s32[]{:S(2)}) async-start(), calls=%async_computation.2 | async-start | bytes 786432 | tf_op jit(solution)/shard_map/while/body/eval_jaxpr/psum | solution.py:24
  2320.7 84.5 %all-reduce.11.cloned.1.call-start = ((), (), s32[]{:S(2)}) async-start(), calls=%async_computation.3 | async-start | bytes 786432 | tf_op jit(solution)/shard_map/while/body/eval_jaxpr/psum | solution.py:24
  2446.0 46.5 %all-reduce.9.cloned.1.call-start = ((), (), s32[]{:S(2)}) async-start(), calls=%async_computation.2 | async-start | bytes 786432 | tf_op jit(solution)/shard_map/while/body/eval_jaxpr/psum | solution.py:24
  2454.8 84.4 %all-reduce.11.cloned.1.call-start = ((), (), s32[]{:S(2)}) async-start(), calls=%async_computation.3 | async-start | bytes 786432 | tf_op jit(solution)/shard_map/while/body/eval_jaxpr/psum | solution.py:24
  (18 other events, 301.6 us)
Sparse Core Ops, SparseCore 0:
  20.0 39.7 all-reduce.4
  68.2 36.8 all-reduce.6
  118.4 40.8 all-reduce.4
  167.7 36.8 all-reduce.6
  217.9 40.8 all-reduce.4
  267.2 36.8 all-reduce.6
  317.3 40.8 all-reduce.4
  366.6 36.8 all-reduce.6
  416.8 40.8 all-reduce.4
  466.1 36.8 all-reduce.6
  516.3 40.8 all-reduce.4
  565.6 36.8 all-reduce.6
  615.7 40.8 all-reduce.4
  665.0 36.8 all-reduce.6
  715.2 40.8 all-reduce.4
  764.5 36.8 all-reduce.6
  814.7 40.8 all-reduce.4
  864.0 36.8 all-reduce.6
  914.1 40.8 all-reduce.4
  963.4 36.8 all-reduce.6
  1013.6 40.8 all-reduce.4
  1062.9 36.8 all-reduce.6
  1124.5 37.5 all-reduce.8
  1171.9 36.8 all-reduce.10
  1249.0 37.6 all-reduce.8
  1296.5 36.8 all-reduce.10
  1383.0 37.6 all-reduce.8
  1430.5 36.8 all-reduce.10
  1517.0 37.6 all-reduce.8
  1564.4 36.8 all-reduce.10
  1651.0 37.6 all-reduce.8
  1698.4 36.8 all-reduce.10
  1785.0 37.6 all-reduce.8
  1832.4 36.8 all-reduce.10
  1918.9 37.6 all-reduce.8
  1966.3 36.8 all-reduce.10
  2052.9 37.6 all-reduce.8
  2100.3 36.8 all-reduce.10
  2186.9 37.6 all-reduce.8
  2234.3 36.8 all-reduce.10
  2320.9 37.6 all-reduce.8
  2368.3 36.8 all-reduce.10
  2454.9 37.6 all-reduce.8
  2502.3 36.8 all-reduce.10
where the time goes:
time: 2590 us
  waiting for transfers between devices  1400 us (54%)
  matrix products  613 us (24%)
  other arithmetic  500 us (19%)
  starting transfers between devices  30.2 us (1%)
    psum x22, waiting for transfers between devices, layer_forward(): branch = lax.psum(partial_sum, 'tp')  846 us
    psum x22, waiting for transfers between devices, layer_backward(): lax.psum(partial_sum, 'tp')  558 us
    add x11, other arithmetic, bwd_tick(): acc_first = acc_first + jnp.stack([first_lower, first_upper])  414 us
    dot_general x22, matrix products, layer_backward(): jnp.einsum('bd,bf->df', h_in, grad_pre, preferred_element_type=jnp.float32)  133 us
    dot_general x22, matrix products, layer_backward(): jnp.einsum('bf,bd->fd', hidden_f.astype(jnp.bfloat16), grad_h, preferred_...  132 us
    dot_general x22, matrix products, layer_backward(): jnp.einsum('bf,df->bd', grad_pre, w_first, preferred_element_type=jnp.flo...  102 us
    dot_general x22, matrix products, layer_forward(): partial_sum = jnp.dot(hidden, w_second, preferred_element_type=jnp.float32)  88.1 us
    dot_general x22, matrix products, layer_backward(): jnp.einsum('bd,fd->bf', grad_h, w_second, preferred_element_type=jnp.floa...  86.6 us
  transfers between devices with their start and end apart: 66, of which 44 were waited for; matrix products, arithmetic and copies ran while one was open for 27% of the time, Pallas kernels for 0%

commit v1 on v0

v1 whole, which is shorter than its diff:
```python
import functools
import math

import jax
import jax.numpy as jnp
from jax import lax
from jax.experimental import pallas as pl
from jax.experimental.pallas import tpu as pltpu
from jax.sharding import PartitionSpec as P

UNIT = 32
N_CHUNK = 2
SLOTS = 4
BLOCK = 512

MESH = pl.DeviceIdType.MESH
F32 = jnp.float32
BF16 = jnp.bfloat16
ROOT = math.sqrt(2 / math.pi)
CUBIC = 0.044715


def gelu_parts(val):
    th = jnp.tanh(ROOT * (val + CUBIC * (val * val * val)))
    cdf = 0.5 * (1.0 + th)
    return val * cdf, cdf + val * (0.5 * (1.0 - th * th) * (ROOT * (1.0 + 3.0 * CUBIC * (val * val))))


def gelu_only(val):
    return val * (0.5 * (1.0 + jnp.tanh(ROOT * (val + CUBIC * (val * val * val)))))


def dot_nn(a, b):
    return jnp.dot(a, b, preferred_element_type=F32)


def dot_nt(a, b):
    return lax.dot_general(a, b, (((1,), (1,)), ((), ())), preferred_element_type=F32)


def pipe_kernel(norm, x_hbm, t_hbm, w1_hbm, w2_hbm,
                h_out, g_out, a_out, e_out, loss_out,
                w1, w2, xs, us, acts, tgt, act_now, part, recv, outb, loss_acc, loss_src, loss_dst,
                w_sem, in_sem, x_sem, part_sem, recv_sem, leaf_sem, peer_sem, copy_sem, loss_sem, loss_got):
    n_stage, n_tp = 4, 4
    _, n, unit, width = xs.shape
    hid = us.shape[3]
    cw = width // N_CHUNK
    stage = lax.axis_index('pp')
    z = lax.axis_index('tp')
    last = n_stage - 1
    is_center = (z == 1) | (z == 2)
    is_leaf = (z == 0) | (z == 3)
    center_i = is_center.astype(jnp.int32)
    partner = z + 1 - 2 * (z % 2)
    peer = partner + center_i * (3 - z - partner)
    at_last_i = (stage == last).astype(jnp.int32)
    gap = 2 - 2 * at_last_i

    w_copies = []
    for k in range(2):
        w_copies.append((pltpu.make_async_copy(w1_hbm.at[k], w1.at[k], w_sem.at[0, k]),
                         pltpu.make_async_copy(w2_hbm.at[k], w2.at[k], w_sem.at[1, k])))
    x_copy = pltpu.make_async_copy(x_hbm, xs.at[0], in_sem.at[0])
    t_copy = pltpu.make_async_copy(t_hbm, tgt, in_sem.at[1])

    @pl.when(stage == 0)
    def _():
        x_copy.start()

    for pair in w_copies:
        for copy in pair:
            copy.start()
    t_copy.start()
    loss_acc[...] = jnp.zeros_like(loss_acc)

    barrier = pltpu.get_barrier_semaphore()
    for ds in range(n_stage):
        for dz in range(n_tp):
            if ds or dz:
                pl.semaphore_signal(barrier, inc=1, device_id={'pp': (stage + ds) % n_stage, 'tp': (z + dz) % n_tp}, device_id_type=MESH)
    pl.semaphore_wait(barrier, n_stage * n_tp - 1)

    @pl.when(stage == 0)
    def _():
        x_copy.wait()

    t_copy.wait()

    def cols(c):
        return pl.ds(c * cw, cw)

    def part_send(p, slot, c):
        return pltpu.make_async_remote_copy(
            src_ref=part.at[p, slot, c], dst_ref=recv.at[center_i, p, slot, c],
            send_sem=part_sem.at[p, slot, c], recv_sem=recv_sem.at[center_i, p, slot, c],
            device_id={'pp': stage, 'tp': peer}, device_id_type=MESH)

    def part_arrival(kind, p, slot, c):
        return pltpu.make_async_remote_copy(
            src_ref=part.at[p, slot, c], dst_ref=recv.at[kind, p, slot, c],
            send_sem=part_sem.at[p, slot, c], recv_sem=recv_sem.at[kind, p, slot, c],
            device_id={'pp': stage, 'tp': peer}, device_id_type=MESH)

    def out_send(p, slot, c, q, m, to_stage, to_tp, sem):
        return pltpu.make_async_remote_copy(
            src_ref=outb.at[p, slot, c], dst_ref=xs.at[q, m, :, cols(c)],
            send_sem=sem.at[p, slot, c], recv_sem=x_sem.at[q, m, c],
            device_id={'pp': to_stage, 'tp': to_tp}, device_id_type=MESH)

    def at(v):
        fwd = (v >= 0) & (v < n)
        bwd = (v >= n + gap) & (v < 2 * n + gap)
        bwd_i = (v >= n).astype(jnp.int32)
        m = v - bwd_i * (n + gap)
        return fwd, bwd, bwd_i, m, m + bwd_i * n

    def arrived(q, m):
        for c in range(N_CHUNK):
            out_send(0, 0, c, q, m, stage, z, leaf_sem).wait_recv()

    def free_part(p, i):
        @pl.when(i >= SLOTS)
        def _():
            for c in range(N_CHUNK):
                part_send(p, i % SLOTS, c).wait_send()

    def send_part(p, slot, c):
        @pl.when(is_leaf)
        def _():
            part_send(p, slot, c).start()

    def compute(v, p):
        fwd, bwd, _, m, i = at(v)
        slot = i % SLOTS

        @pl.when(fwd)
        def _():
            @pl.when(m == 0)
            def _():
                w_copies[p][0].wait()
            if p == 0:
                @pl.when(stage > 0)
                def _():
                    arrived(0, m)
            else:
                @pl.when(is_leaf)
                def _():
                    arrived(1, m)
            free_part(p, i)
            for j in range(hid // BLOCK):
                js = pl.ds(j * BLOCK, BLOCK)
                pre = dot_nn(xs[p, m], w1[p, :, js]).astype(BF16)
                us[p, m, :, js] = pre
                act_now[:, js] = gelu_only(pre.astype(F32)).astype(BF16)

            @pl.when(m == 0)
            def _():
                w_copies[p][1].wait()
            for c in range(N_CHUNK):
                part[p, slot, c] = dot_nn(act_now[...], w2[p, :, cols(c)])
                send_part(p, slot, c)

        @pl.when(bwd)
        def _():
            k = 1 - p
            if p == 0:
                @pl.when(is_leaf | (stage < last))
                def _():
                    arrived(2, m)
            else:
                @pl.when(is_leaf)
                def _():
                    arrived(3, m)

            def outs():
                return (pltpu.make_async_copy(xs.at[k, m], h_out.at[k, m], copy_sem.at[p, 0]),
                        pltpu.make_async_copy(xs.at[2 + p, m], g_out.at[k, m], copy_sem.at[p, 1]),
                        pltpu.make_async_copy(acts.at[k, m], a_out.at[k, m], copy_sem.at[p, 2]),
                        pltpu.make_async_copy(us.at[k, m], e_out.at[k, m], copy_sem.at[p, 3]))

            @pl.when(m > 0)
            def _():
                for copy in outs():
                    copy.wait()
            for j in range(hid // BLOCK):
                js = pl.ds(j * BLOCK, BLOCK)
                grad = dot_nt(xs[2 + p, m], w2[k, js, :])
                act, slope = gelu_parts(us[k, m, :, js].astype(F32))
                acts[k, m, :, js] = act.astype(BF16)
                err = (slope * grad).astype(BF16)
                us[k, m, :, js] = err
                act_now[:, js] = err

            def down():
                free_part(p, i)
                for c in range(N_CHUNK):
                    part[p, slot, c] = dot_nt(act_now[...], w1[k, cols(c), :])
                    send_part(p, slot, c)

            if p == 0:
                down()
            else:
                pl.when(stage > 0)(down)
            for copy in outs():
                copy.start()

    def sums(v, p):
        fwd, bwd, bwd_i, m, i = at(v)
        live = fwd | bwd if p == 0 else fwd | (bwd & (stage > 0))
        return live & is_center, fwd, bwd_i, m, i, i % SLOTS

    def add_leaf(v, p):
        live, _, _, _, _, slot = sums(v, p)

        @pl.when(live)
        def _():
            for c in range(N_CHUNK):
                part_arrival(0, p, slot, c).wait_recv()
                part[p, slot, c] = part[p, slot, c] + recv[0, p, slot, c]
                part_send(p, slot, c).start()

    def finish(v, p):
        live, fwd, bwd_i, m, i, slot = sums(v, p)
        if p == 0:
            to_stage, q = stage, 1 + 2 * bwd_i
        else:
            home = (1 - bwd_i) * at_last_i
            to_stage, q = stage + (1 - home) * (1 - 2 * bwd_i), 2 * bwd_i + 2 * home

        @pl.when(live)
        def _():
            @pl.when(i >= SLOTS)
            def _():
                for c in range(N_CHUNK):
                    out_send(p, slot, c, q, m, to_stage, partner, leaf_sem).wait_send()
            if p == 1:
                @pl.when((i >= SLOTS) & ((stage < last) | (i >= SLOTS + n)))
                def _():
                    for c in range(N_CHUNK):
                        out_send(p, slot, c, q, m, to_stage, z, peer_sem).wait_send()
            for c in range(N_CHUNK):
                part_arrival(1, p, slot, c).wait_recv()
                res = (xs[2 * bwd_i + p, m, :, cols(c)].astype(F32) + (part[p, slot, c] + recv[1, p, slot, c])).astype(BF16)
                if p == 0:
                    outb[p, slot, c] = res
                    xs[q, m, :, cols(c)] = res
                else:
                    @pl.when((stage < last) | (bwd_i == 1))
                    def _():
                        outb[p, slot, c] = res
                        out_send(p, slot, c, q, m, to_stage, z, peer_sem).start()

                    @pl.when((stage == last) & (bwd_i == 0))
                    def _():
                        diff = res.astype(F32) - tgt[m, :, cols(c)].astype(F32)
                        grad = (diff * norm).astype(BF16)
                        outb[p, slot, c] = grad
                        xs[q, m, :, cols(c)] = grad
                        sq = diff * diff
                        acc = loss_acc[...]
                        for r in range(unit // 8):
                            for b in range(cw // 128):
                                acc = acc + sq[r * 8:(r + 1) * 8, b * 128:(b + 1) * 128]
                        loss_acc[...] = acc
                out_send(p, slot, c, q, m, to_stage, partner, leaf_sem).start()

    def step(t, carry):
        compute(t, 0)
        add_leaf(t - 2, 1)
        finish(t - 1, 0)
        compute(t - 1, 1)
        add_leaf(t, 0)
        finish(t - 2, 1)
        return carry

    lax.fori_loop(0, 2 * n + 4, step, 0)

    for p in range(2):
        for slot in range(SLOTS):
            for c in range(N_CHUNK):
                part_send(p, slot, c).wait_send()

                @pl.when(is_center)
                def _():
                    out_send(p, slot, c, 0, 0, stage, partner, leaf_sem).wait_send()
                    if p == 1:
                        out_send(p, slot, c, 0, 0, stage, z, peer_sem).wait_send()
        k = 1 - p
        pltpu.make_async_copy(xs.at[k, 0], h_out.at[k, 0], copy_sem.at[p, 0]).wait()
        pltpu.make_async_copy(xs.at[2 + p, 0], g_out.at[k, 0], copy_sem.at[p, 1]).wait()
        pltpu.make_async_copy(acts.at[k, 0], a_out.at[k, 0], copy_sem.at[p, 2]).wait()
        pltpu.make_async_copy(us.at[k, 0], e_out.at[k, 0], copy_sem.at[p, 3]).wait()

    def loss_send(idx, to_stage, to_tp):
        return pltpu.make_async_remote_copy(
            src_ref=loss_src, dst_ref=loss_dst, send_sem=loss_sem.at[idx], recv_sem=loss_got.at[0],
            device_id={'pp': to_stage, 'tp': to_tp}, device_id_type=MESH)

    sender = is_center & (stage == last)

    @pl.when(sender)
    def _():
        total = jnp.sum(loss_acc[...]) * 0.5 * norm
        value = jnp.full(loss_src.shape, total, F32)
        loss_src[...] = value
        loss_out[...] = value
        sends = [loss_send(2 * s + b, s, z if b else partner) for s in range(n_stage) for b in range(2) if not (s == last and b)]
        for send in sends:
            send.start()
        for send in sends:
            send.wait_send()

    @pl.when(is_leaf | (stage < last))
    def _():
        loss_send(0, stage, z).wait_recv()
        loss_out[...] = loss_dst[...]


def solution(mesh):
    def stage_body(x_micro, targets, w_in, w_out):
        n_micro, n_token, width = x_micro.shape
        hid = w_in.shape[3]
        n = n_micro * n_token // UNIT
        norm = 1.0 / (n_micro * n_token * width)
        cw = width // N_CHUNK
        any_spec = pl.BlockSpec(memory_space=pl.ANY)
        h, g, a, e, loss = pl.pallas_call(
            functools.partial(pipe_kernel, norm),
            out_shape=(
                jax.ShapeDtypeStruct((2, n, UNIT, width), BF16),
                jax.ShapeDtypeStruct((2, n, UNIT, width), BF16),
                jax.ShapeDtypeStruct((2, n, UNIT, hid), BF16),
                jax.ShapeDtypeStruct((2, n, UNIT, hid), BF16),
                jax.ShapeDtypeStruct((8, 128), F32),
            ),
            in_specs=[any_spec] * 4,
            out_specs=(any_spec, any_spec, any_spec, any_spec, pl.BlockSpec(memory_space=pltpu.VMEM)),
            scratch_shapes=[
                pltpu.VMEM((2, width, hid), BF16),
                pltpu.VMEM((2, hid, width), BF16),
                pltpu.VMEM((4, n, UNIT, width), BF16),
                pltpu.VMEM((2, n, UNIT, hid), BF16),
                pltpu.VMEM((2, n, UNIT, hid), BF16),
                pltpu.VMEM((n, UNIT, width), BF16),
                pltpu.VMEM((UNIT, hid), BF16),
                pltpu.VMEM((2, SLOTS, N_CHUNK, UNIT, cw), F32),
                pltpu.VMEM((2, 2, SLOTS, N_CHUNK, UNIT, cw), F32),
                pltpu.VMEM((2, SLOTS, N_CHUNK, UNIT, cw), BF16),
                pltpu.VMEM((8, 128), F32),
                pltpu.VMEM((8, 128), F32),
                pltpu.VMEM((8, 128), F32),
                pltpu.SemaphoreType.DMA((2, 2)),
                pltpu.SemaphoreType.DMA((2,)),
                pltpu.SemaphoreType.DMA((4, n, N_CHUNK)),
                pltpu.SemaphoreType.DMA((2, SLOTS, N_CHUNK)),
                pltpu.SemaphoreType.DMA((2, 2, SLOTS, N_CHUNK)),
                pltpu.SemaphoreType.DMA((2, SLOTS, N_CHUNK)),
                pltpu.SemaphoreType.DMA((2, SLOTS, N_CHUNK)),
                pltpu.SemaphoreType.DMA((2, 4)),
                pltpu.SemaphoreType.DMA((8,)),
                pltpu.SemaphoreType.DMA((1,)),
            ],
            compiler_params=pltpu.CompilerParams(collective_id=0, has_side_effects=True, vmem_limit_bytes=60 * 1024 * 1024),
        )(x_micro.reshape(n, UNIT, width), targets.reshape(n, UNIT, width), w_in[0], w_out[0])

        h, g = (v.reshape(2, n * UNIT, width) for v in (h, g))
        a, e = (v.reshape(2, n * UNIT, hid) for v in (a, e))
        grad_first = jnp.einsum('kbd,kbf->kdf', h, e, preferred_element_type=F32)
        grad_second = jnp.einsum('kbf,kbd->kfd', a, g, preferred_element_type=F32)
        return grad_first[None], grad_second[None], loss[0, :1]

    data_spec = P('dp', None, None)
    return jax.shard_map(stage_body, mesh=mesh, in_specs=(data_spec, data_spec, P('pp', None, None, 'tp'), P('pp', None, 'tp', None)), out_specs=(P(('dp', 'pp'), None, None, 'tp'), P(('dp', 'pp'), None, 'tp', None), P('dp')), check_vma=False)
```

time: 2590 us -> 544 us (0.21)
  waiting for transfers between devices: 1400 us -> 0 us
  matrix products: 613 us -> 21.6 us
  Pallas kernels: 0 us -> 521 us
  other arithmetic: 500 us -> 0 us
  starting transfers between devices: 30.2 us -> 0 us
    psum x44 -> x0, waiting for transfers between devices: 1400 us -> none  [the longest x22 846 us: layer_forward(): branch = lax.psum(partial_sum, 'tp')]
    dot_general x132 -> x2, matrix products: 613 us -> 21.6 us  [the longest x1 12 us: stage_body(): grad_first = jnp.einsum('kbd,kbf->kdf', h, e, preferred_element_type=F32)]
    pallas_call x0 -> x1, Pallas kernels: none -> 521 us  [stage_body(): pl.pallas_call(functools.partial(pipe_kernel, norm), out_shape=(jax.Shape...]
    add x11 -> x0, other arithmetic: 414 us -> none  [bwd_tick(): acc_first = acc_first + jnp.stack([first_lower, first_upper])]
    convert_element_type x33 -> x0, other arithmetic: 34 us -> none  [the longest x22 22.7 us: layer_backward(): (grad_h.astype(jnp.float32) + lax.psum(partial_sum, 'tp')).astype(jnp.bfl...]
    ppermute x22 -> x0, starting transfers between devices: 28.4 us -> none  [the longest x11 14.2 us: bwd_tick(): received = lax.ppermute(grad_in, 'pp', send_up)]
  transfers between devices with their start and end apart: 66 -> 0, of which waited for: 44 -> 0; matrix products, arithmetic and copies ran while one was open for 27% -> 0% of each run, Pallas kernels for 0% -> 0%
where the time goes in v1:
time: 544 us
  Pallas kernels  521 us (96%)
  matrix products  21.6 us (4%)
    pallas_call x1, Pallas kernels, stage_body(): pl.pallas_call(functools.partial(pipe_kernel, norm), out_shape=(jax.Shape...  521 us
    dot_general x1, matrix products, stage_body(): grad_first = jnp.einsum('kbd,kbf->kdf', h, e, preferred_element_type=F32)  12 us

profile of v1, /device:TPU:0, one launch (start us, length us, event | category | flops | bytes accessed | tf_op | source)
XLA Modules:
  0.0 544.1 jit_solution(12094748024423024509)
XLA Ops:
  0.6 520.7 %shard_map.67 = (bf16[2,16,32,1536]{3,2,1,0:T(8,128)(2,1)}, bf16[2,16,32,1536]{3,2,1,0:T(8,128)(2,1)}, bf16[2,16,32,1536]{3,2,1,0:T(8,128)(2,1)}, bf16[2,16,32,1536]{3,2,1,0:T(8,128)(2,1)}, f32[8,128]{1,0:T(8,128)}) custom-call(bf16[16,32,1536]{2,1,0:T(8,128)(2,1)} %bitcast.19, bf16[16,32,1536]{2,1,0:T(8,128)(2,1)} %bitcast.20, ...), custom_call_target="tpu_custom_call" | custom-call | tf_op jit(solution)/shard_map/pallas_call | solution.py:328
  521.4 1.2 slice.3
  522.6 0.0 copy-start
  522.6 0.0 copy-start.1
  522.6 12.0 %convolution_bitcast_fusion.1 = f32[1,2,1536,1536]{3,2,1,0:T(8,128)} fusion(bf16[2,512,1536]{2,1,0:T(8,128)(2,1)} %bitcast.23, bf16[2,512,1536]{2,1,0:T(8,128)(2,1)} %bitcast.24), kind=kOutput, calls=%fused_computation.1 | convolution fusion | flops 4831838208 | bytes 25165824 | tf_op jit(solution)/shard_map/kbd,kbf->kdf/dot_general | solution.py:369
  534.6 0.0 copy-done
  534.6 0.0 copy-done.1
  534.6 9.5 %convolution_bitcast_fusion = f32[1,2,1536,1536]{3,2,1,0:T(8,128)} fusion(bf16[2,512,1536]{2,1,0:T(8,128)(2,1)S(1)} %bitcast.22, bf16[2,512,1536]{2,1,0:T(8,128)(2,1)S(1)} %bitcast.21), kind=kOutput, calls=%fused_computation | convolution fusion | flops 4831838208 | bytes 25165824 | tf_op jit(solution)/shard_map/kbf,kbd->kfd/dot_general | solution.py:370
Async XLA Ops:
  522.6 12.0 %copy-start = (bf16[2,16,32,1536]{3,2,1,0:T(8,128)(2,1)S(1)}, bf16[2,16,32,1536]{3,2,1,0:T(8,128)(2,1)}, u32[]{:S(2)}) copy-start(bf16[2,16,32,1536]{3,2,1,0:T(8,128)(2,1)} %get-tuple-element.11) | copy-start | bytes 9437188
  522.6 12.0 %copy-start.1 = (bf16[2,16,32,1536]{3,2,1,0:T(8,128)(2,1)S(1)}, bf16[2,16,32,1536]{3,2,1,0:T(8,128)(2,1)}, u32[]{:S(2)}) copy-start(bf16[2,16,32,1536]{3,2,1,0:T(8,128)(2,1)} %get-tuple-element.10) | copy-start | bytes 9437188

commit v2 on v1

--- a/solution.py
+++ b/solution.py
@@ -9,9 +9,10 @@
 from jax.sharding import PartitionSpec as P
 
 UNIT = 32
-N_CHUNK = 2
+N_CHUNK = 3
 SLOTS = 4
 BLOCK = 512
+GAP = 3
 
 MESH = pl.DeviceIdType.MESH
 F32 = jnp.float32
@@ -55,7 +56,7 @@
     partner = z + 1 - 2 * (z % 2)
     peer = partner + center_i * (3 - z - partner)
     at_last_i = (stage == last).astype(jnp.int32)
-    gap = 2 - 2 * at_last_i
+    gap = GAP * (1 - at_last_i)
 
     w_copies = []
     for k in range(2):
@@ -85,7 +86,9 @@
     def _():
         x_copy.wait()
 
-    t_copy.wait()
+    @pl.when(stage == last)
+    def _():
+        t_copy.wait()
 
     def cols(c):
         return pl.ds(c * cw, cw)
@@ -266,15 +269,19 @@
                 out_send(p, slot, c, q, m, to_stage, partner, leaf_sem).start()
 
     def step(t, carry):
+        compute(t - 3 + center_i, 1)
         compute(t, 0)
+        finish(t - 1, 0)
+        add_leaf(t, 0)
+        finish(t - 3, 1)
         add_leaf(t - 2, 1)
-        finish(t - 1, 0)
-        compute(t - 1, 1)
-        add_leaf(t, 0)
-        finish(t - 2, 1)
         return carry
 
-    lax.fori_loop(0, 2 * n + 4, step, 0)
+    lax.fori_loop(0, 2 * n + GAP + 3, step, 0)
+
+    @pl.when(stage < last)
+    def _():
+        t_copy.wait()
 
     for p in range(2):
         for slot in range(SLOTS):

time: 544 us -> 506 us (0.930)
  Pallas kernels: 521 us -> 482 us
    pallas_call x1, Pallas kernels: 521 us -> 482 us  [stage_body(): pl.pallas_call(functools.partial(pipe_kernel, norm), out_shape=(jax.Shape...]
where the time goes in v2:
time: 506 us; the launch traced here: 505 us
  Pallas kernels  482 us (95%)
  matrix products  21.6 us (4%)
    pallas_call x1, Pallas kernels, stage_body(): pl.pallas_call(functools.partial(pipe_kernel, norm), out_shape=(jax.Shape...  482 us
    dot_general x1, matrix products, stage_body(): grad_first = jnp.einsum('kbd,kbf->kdf', h, e, preferred_element_type=F32)  12 us

profile of v2, /device:TPU:0, one launch (start us, length us, event | category | flops | bytes accessed | tf_op | source)
XLA Modules:
  0.0 505.3 jit_solution(1535966760283080697)
XLA Ops:
  0.6 482.0 %shard_map.67 = (bf16[2,16,32,1536]{3,2,1,0:T(8,128)(2,1)}, bf16[2,16,32,1536]{3,2,1,0:T(8,128)(2,1)}, bf16[2,16,32,1536]{3,2,1,0:T(8,128)(2,1)}, bf16[2,16,32,1536]{3,2,1,0:T(8,128)(2,1)}, f32[8,128]{1,0:T(8,128)}) custom-call(bf16[16,32,1536]{2,1,0:T(8,128)(2,1)} %bitcast.19, bf16[16,32,1536]{2,1,0:T(8,128)(2,1)} %bitcast.20, ...), custom_call_target="tpu_custom_call" | custom-call | tf_op jit(solution)/shard_map/pallas_call | solution.py:335
  482.6 1.2 slice.3
  483.8 0.0 copy-start
  483.8 0.0 copy-start.1
  483.8 12.0 %convolution_bitcast_fusion.1 = f32[1,2,1536,1536]{3,2,1,0:T(8,128)} fusion(bf16[2,512,1536]{2,1,0:T(8,128)(2,1)} %bitcast.23, bf16[2,512,1536]{2,1,0:T(8,128)(2,1)} %bitcast.24), kind=kOutput, calls=%fused_computation.1 | convolution fusion | flops 4831838208 | bytes 25165824 | tf_op jit(solution)/shard_map/kbd,kbf->kdf/dot_general | solution.py:376
  495.8 0.0 copy-done
  495.8 0.0 copy-done.1
  495.8 9.5 %convolution_bitcast_fusion = f32[1,2,1536,1536]{3,2,1,0:T(8,128)} fusion(bf16[2,512,1536]{2,1,0:T(8,128)(2,1)S(1)} %bitcast.22, bf16[2,512,1536]{2,1,0:T(8,128)(2,1)S(1)} %bitcast.21), kind=kOutput, calls=%fused_computation | convolution fusion | flops 4831838208 | bytes 25165824 | tf_op jit(solution)/shard_map/kbf,kbd->kfd/dot_general | solution.py:377
Async XLA Ops:
  483.8 12.0 %copy-start = (bf16[2,16,32,1536]{3,2,1,0:T(8,128)(2,1)S(1)}, bf16[2,16,32,1536]{3,2,1,0:T(8,128)(2,1)}, u32[]{:S(2)}) copy-start(bf16[2,16,32,1536]{3,2,1,0:T(8,128)(2,1)} %get-tuple-element.11) | copy-start | bytes 9437188
  483.8 12.0 %copy-start.1 = (bf16[2,16,32,1536]{3,2,1,0:T(8,128)(2,1)S(1)}, bf16[2,16,32,1536]{3,2,1,0:T(8,128)(2,1)}, u32[]{:S(2)}) copy-start(bf16[2,16,32,1536]{3,2,1,0:T(8,128)(2,1)} %get-tuple-element.10) | copy-start | bytes 9437188

commit v3 on v2

--- a/solution.py
+++ b/solution.py
@@ -12,7 +12,8 @@
 N_CHUNK = 3
 SLOTS = 4
 BLOCK = 512
-GAP = 3
+TILE = 256
+GAP = 4
 
 MESH = pl.DeviceIdType.MESH
 F32 = jnp.float32
@@ -21,6 +22,12 @@
 CUBIC = 0.044715
 
 
+ALL = tuple(range(N_CHUNK))
+ORDER = (('sum', 3, 1, (1,)), ('dot', 0, 0, ALL), ('sum', 3, 1, (2,)), ('end', 1, 0, (1, 0)), ('sum', 0, 0, (0, 1)), ('end', 1, 0, (2,)),
+         ('dot', 1, 1, ALL), ('end', 3, 1, (0,)), ('sum', 0, 0, (2,)), ('end', 3, 1, (1,)), ('sum', 2, 1, (0,)), ('end', 3, 1, (2,)))
+OUTER_LAG = 2
+
+
 def gelu_parts(val):
     th = jnp.tanh(ROOT * (val + CUBIC * (val * val * val)))
     cdf = 0.5 * (1.0 + th)
@@ -35,13 +42,9 @@
     return jnp.dot(a, b, preferred_element_type=F32)
 
 
-def dot_nt(a, b):
-    return lax.dot_general(a, b, (((1,), (1,)), ((), ())), preferred_element_type=F32)
-
-
 def pipe_kernel(norm, x_hbm, t_hbm, w1_hbm, w2_hbm,
                 h_out, g_out, a_out, e_out, loss_out,
-                w1, w2, xs, us, acts, tgt, act_now, part, recv, outb, loss_acc, loss_src, loss_dst,
+                w1, w2, w1t, w2t, xs, us, acts, tgt, act_now, part, recv, outb, loss_acc, loss_src, loss_dst,
                 w_sem, in_sem, x_sem, part_sem, recv_sem, leaf_sem, peer_sem, copy_sem, loss_sem, loss_got):
     n_stage, n_tp = 4, 4
     _, n, unit, width = xs.shape
@@ -90,6 +93,27 @@
     def _():
         t_copy.wait()
 
+    def flip():
+        for src, dst in ((w1, w1t), (w2, w2t)):
+            _, rows, columns = src.shape
+
+            def tile_row(i, carry):
+                k = i // (rows // TILE)
+                at_row = pl.ds(pl.multiple_of((i % (rows // TILE)) * TILE, TILE), TILE)
+                for j in range(columns // TILE):
+                    js = pl.ds(j * TILE, TILE)
+                    dst[k, js, at_row] = src[k, at_row, js].T
+                return carry
+
+            lax.fori_loop(0, 2 * (rows // TILE), tile_row, 0)
+
+    @pl.when(stage > 0)
+    def _():
+        for pair in w_copies:
+            for copy in pair:
+                copy.wait()
+        flip()
+
     def cols(c):
         return pl.ds(c * cw, cw)
 
@@ -139,7 +163,7 @@
 
         @pl.when(fwd)
         def _():
-            @pl.when(m == 0)
+            @pl.when((m == 0) & (stage == 0))
             def _():
                 w_copies[p][0].wait()
             if p == 0:
@@ -157,7 +181,7 @@
                 us[p, m, :, js] = pre
                 act_now[:, js] = gelu_only(pre.astype(F32)).astype(BF16)
 
-            @pl.when(m == 0)
+            @pl.when((m == 0) & (stage == 0))
             def _():
                 w_copies[p][1].wait()
             for c in range(N_CHUNK):
@@ -188,7 +212,7 @@
                     copy.wait()
             for j in range(hid // BLOCK):
                 js = pl.ds(j * BLOCK, BLOCK)
-                grad = dot_nt(xs[2 + p, m], w2[k, js, :])
+                grad = dot_nn(xs[2 + p, m], w2t[k, :, js])
                 act, slope = gelu_parts(us[k, m, :, js].astype(F32))
                 acts[k, m, :, js] = act.astype(BF16)
                 err = (slope * grad).astype(BF16)
@@ -198,7 +222,7 @@
             def down():
                 free_part(p, i)
                 for c in range(N_CHUNK):
-                    part[p, slot, c] = dot_nt(act_now[...], w1[k, cols(c), :])
+                    part[p, slot, c] = dot_nn(act_now[...], w1t[k, :, cols(c)])
                     send_part(p, slot, c)
 
             if p == 0:
@@ -213,17 +237,17 @@
         live = fwd | bwd if p == 0 else fwd | (bwd & (stage > 0))
         return live & is_center, fwd, bwd_i, m, i, i % SLOTS
 
-    def add_leaf(v, p):
+    def add_leaf(v, p, chunks):
         live, _, _, _, _, slot = sums(v, p)
 
         @pl.when(live)
         def _():
-            for c in range(N_CHUNK):
+            for c in chunks:
                 part_arrival(0, p, slot, c).wait_recv()
                 part[p, slot, c] = part[p, slot, c] + recv[0, p, slot, c]
                 part_send(p, slot, c).start()
 
-    def finish(v, p):
+    def finish(v, p, chunks):
         live, fwd, bwd_i, m, i, slot = sums(v, p)
         if p == 0:
             to_stage, q = stage, 1 + 2 * bwd_i
@@ -235,14 +259,14 @@
         def _():
             @pl.when(i >= SLOTS)
             def _():
-                for c in range(N_CHUNK):
+                for c in chunks:
                     out_send(p, slot, c, q, m, to_stage, partner, leaf_sem).wait_send()
             if p == 1:
                 @pl.when((i >= SLOTS) & ((stage < last) | (i >= SLOTS + n)))
                 def _():
-                    for c in range(N_CHUNK):
+                    for c in chunks:
                         out_send(p, slot, c, q, m, to_stage, z, peer_sem).wait_send()
-            for c in range(N_CHUNK):
+            for c in chunks:
                 part_arrival(1, p, slot, c).wait_recv()
                 res = (xs[2 * bwd_i + p, m, :, cols(c)].astype(F32) + (part[p, slot, c] + recv[1, p, slot, c])).astype(BF16)
                 if p == 0:
@@ -269,12 +293,17 @@
                 out_send(p, slot, c, q, m, to_stage, partner, leaf_sem).start()
 
     def step(t, carry):
-        compute(t - 3 + center_i, 1)
-        compute(t, 0)
-        finish(t - 1, 0)
-        add_leaf(t, 0)
-        finish(t - 3, 1)
-        add_leaf(t - 2, 1)
+        @pl.when((stage == 0) & (t == n + GAP - 1))
+        def _():
+            flip()
+
+        for kind, lag, p, chunks in ORDER:
+            if kind == 'dot':
+                compute(t - lag - p * (OUTER_LAG - lag) * (1 - center_i), p)
+            elif kind == 'sum':
+                add_leaf(t - lag, p, chunks)
+            else:
+                finish(t - lag, p, chunks)
         return carry
 
     lax.fori_loop(0, 2 * n + GAP + 3, step, 0)
@@ -346,6 +375,8 @@
             scratch_shapes=[
                 pltpu.VMEM((2, width, hid), BF16),
                 pltpu.VMEM((2, hid, width), BF16),
+                pltpu.VMEM((2, hid, width), BF16),
+                pltpu.VMEM((2, width, hid), BF16),
                 pltpu.VMEM((4, n, UNIT, width), BF16),
                 pltpu.VMEM((2, n, UNIT, hid), BF16),
                 pltpu.VMEM((2, n, UNIT, hid), BF16),
@@ -368,7 +399,7 @@
                 pltpu.SemaphoreType.DMA((8,)),
                 pltpu.SemaphoreType.DMA((1,)),
             ],
-            compiler_params=pltpu.CompilerParams(collective_id=0, has_side_effects=True, vmem_limit_bytes=60 * 1024 * 1024),
+            compiler_params=pltpu.CompilerParams(collective_id=0, has_side_effects=True, vmem_limit_bytes=67043328),
         )(x_micro.reshape(n, UNIT, width), targets.reshape(n, UNIT, width), w_in[0], w_out[0])
 
         h, g = (v.reshape(2, n * UNIT, width) for v in (h, g))

time: 506 us -> 461 us (0.911)
  Pallas kernels: 482 us -> 438 us
    pallas_call x1, Pallas kernels: 482 us -> 438 us  [stage_body(): pl.pallas_call(functools.partial(pipe_kernel, norm), out_shape=(jax.Shape...]
where the time goes in v3:
time: 461 us
  Pallas kernels  438 us (95%)
  matrix products  21.6 us (5%)
    pallas_call x1, Pallas kernels, stage_body(): pl.pallas_call(functools.partial(pipe_kernel, norm), out_shape=(jax.Shape...  438 us
    dot_general x1, matrix products, stage_body(): grad_first = jnp.einsum('kbd,kbf->kdf', h, e, preferred_element_type=F32)  12 us
    dot_general x1, matrix products, stage_body(): grad_second = jnp.einsum('kbf,kbd->kfd', a, g, preferred_element_type=F32)  9.53 us

profile of v3, /device:TPU:0, one launch (start us, length us, event | category | flops | bytes accessed | tf_op | source)
XLA Modules:
  0.0 461.1 jit_solution(7218118039944848289)
XLA Ops:
  0.6 437.7 %shard_map.67 = (bf16[2,16,32,1536]{3,2,1,0:T(8,128)(2,1)}, bf16[2,16,32,1536]{3,2,1,0:T(8,128)(2,1)}, bf16[2,16,32,1536]{3,2,1,0:T(8,128)(2,1)}, bf16[2,16,32,1536]{3,2,1,0:T(8,128)(2,1)}, f32[8,128]{1,0:T(8,128)}) custom-call(bf16[16,32,1536]{2,1,0:T(8,128)(2,1)} %bitcast.19, bf16[16,32,1536]{2,1,0:T(8,128)(2,1)} %bitcast.20, ...), custom_call_target="tpu_custom_call" | custom-call | tf_op jit(solution)/shard_map/pallas_call | solution.py:364
  438.3 1.2 slice.3
  439.5 0.0 copy-start
  439.5 0.0 copy-start.1
  439.5 12.0 %convolution_bitcast_fusion.1 = f32[1,2,1536,1536]{3,2,1,0:T(8,128)} fusion(bf16[2,512,1536]{2,1,0:T(8,128)(2,1)} %bitcast.23, bf16[2,512,1536]{2,1,0:T(8,128)(2,1)} %bitcast.24), kind=kOutput, calls=%fused_computation.1 | convolution fusion | flops 4831838208 | bytes 25165824 | tf_op jit(solution)/shard_map/kbd,kbf->kdf/dot_general | solution.py:407
  451.5 0.0 copy-done
  451.5 0.0 copy-done.1
  451.5 9.5 %convolution_bitcast_fusion = f32[1,2,1536,1536]{3,2,1,0:T(8,128)} fusion(bf16[2,512,1536]{2,1,0:T(8,128)(2,1)S(1)} %bitcast.22, bf16[2,512,1536]{2,1,0:T(8,128)(2,1)S(1)} %bitcast.21), kind=kOutput, calls=%fused_computation | convolution fusion | flops 4831838208 | bytes 25165824 | tf_op jit(solution)/shard_map/kbf,kbd->kfd/dot_general | solution.py:408
Async XLA Ops:
  439.5 12.0 %copy-start = (bf16[2,16,32,1536]{3,2,1,0:T(8,128)(2,1)S(1)}, bf16[2,16,32,1536]{3,2,1,0:T(8,128)(2,1)}, u32[]{:S(2)}) copy-start(bf16[2,16,32,1536]{3,2,1,0:T(8,128)(2,1)} %get-tuple-element.11) | copy-start | bytes 9437188
  439.5 12.0 %copy-start.1 = (bf16[2,16,32,1536]{3,2,1,0:T(8,128)(2,1)S(1)}, bf16[2,16,32,1536]{3,2,1,0:T(8,128)(2,1)}, u32[]{:S(2)}) copy-start(bf16[2,16,32,1536]{3,2,1,0:T(8,128)(2,1)} %get-tuple-element.10) | copy-start | bytes 9437188

commit v4 on v3

--- a/solution.py
+++ b/solution.py
@@ -12,6 +12,7 @@
 N_CHUNK = 3
 SLOTS = 4
 BLOCK = 512
+GRAD_BLOCKS = 3
 TILE = 256
 GAP = 4
 
@@ -72,10 +73,8 @@
     def _():
         x_copy.start()
 
-    for pair in w_copies:
-        for copy in pair:
-            copy.start()
-    t_copy.start()
+    for copy in w_copies[0]:
+        copy.start()
     loss_acc[...] = jnp.zeros_like(loss_acc)
 
     barrier = pltpu.get_barrier_semaphore()
@@ -84,6 +83,10 @@
             if ds or dz:
                 pl.semaphore_signal(barrier, inc=1, device_id={'pp': (stage + ds) % n_stage, 'tp': (z + dz) % n_tp}, device_id_type=MESH)
     pl.semaphore_wait(barrier, n_stage * n_tp - 1)
+
+    for copy in w_copies[1]:
+        copy.start()
+    t_copy.start()
 
     @pl.when(stage == 0)
     def _():
@@ -351,6 +354,22 @@
     def _():
         loss_send(0, stage, z).wait_recv()
         loss_out[...] = loss_dst[...]
+
+
+def weight_grads(h_ref, e_ref, a_ref, g_ref, loss_ref, first_ref, second_ref, total_ref):
+    half = pl.program_id(0)
+
+    def over_tokens(left, right):
+        return lax.dot_general(left, right, (((0,), (0,)), ((), ())), preferred_element_type=F32)
+
+    @pl.when(half == 0)
+    def _():
+        total_ref[0] = jnp.max(loss_ref[...])
+        first_ref[0] = over_tokens(h_ref[0], e_ref[0])
+
+    @pl.when(half == 1)
+    def _():
+        second_ref[0] = over_tokens(a_ref[0], g_ref[0])
 
 
 def solution(mesh):
@@ -404,9 +423,30 @@
 
         h, g = (v.reshape(2, n * UNIT, width) for v in (h, g))
         a, e = (v.reshape(2, n * UNIT, hid) for v in (a, e))
-        grad_first = jnp.einsum('kbd,kbf->kdf', h, e, preferred_element_type=F32)
-        grad_second = jnp.einsum('kbf,kbd->kfd', a, g, preferred_element_type=F32)
-        return grad_first[None], grad_second[None], loss[0, :1]
+        tokens = n * UNIT
+        grad_first, grad_second, total = pl.pallas_call(
+            weight_grads,
+            grid=(2, 2, GRAD_BLOCKS),
+            out_shape=(
+                jax.ShapeDtypeStruct((2, width, hid), F32),
+                jax.ShapeDtypeStruct((2, hid, width), F32),
+                jax.ShapeDtypeStruct((1,), F32),
+            ),
+            in_specs=[
+                pl.BlockSpec((1, tokens, width), lambda i, k, j: (k + i * (1 - k), 0, 0)),
+                pl.BlockSpec((1, tokens, hid // GRAD_BLOCKS), lambda i, k, j: (k + i * (1 - k), 0, j + i * (GRAD_BLOCKS - 1 - j))),
+                pl.BlockSpec((1, tokens, hid), lambda i, k, j: (k * i, 0, 0)),
+                pl.BlockSpec((1, tokens, width // GRAD_BLOCKS), lambda i, k, j: (k * i, 0, j * i)),
+                pl.BlockSpec(memory_space=pltpu.VMEM),
+            ],
+            out_specs=(
+                pl.BlockSpec((1, width, hid // GRAD_BLOCKS), lambda i, k, j: (k + i * (1 - k), 0, j + i * (GRAD_BLOCKS - 1 - j))),
+                pl.BlockSpec((1, hid, width // GRAD_BLOCKS), lambda i, k, j: (k * i, 0, j * i)),
+                pl.BlockSpec(memory_space=pltpu.SMEM),
+            ),
+            compiler_params=pltpu.CompilerParams(vmem_limit_bytes=56 * 1024 * 1024),
+        )(h, e, a, g, loss)
+        return grad_first[None], grad_second[None], total
 
     data_spec = P('dp', None, None)
     return jax.shard_map(stage_body, mesh=mesh, in_specs=(data_spec, data_spec, P('pp', None, None, 'tp'), P('pp', None, 'tp', None)), out_specs=(P(('dp', 'pp'), None, None, 'tp'), P(('dp', 'pp'), None, 'tp', None), P('dp')), check_vma=False)

time: 461 us -> 460 us (level)
  matrix products: 21.6 us -> 0 us
  Pallas kernels: 438 us -> 459 us
    pallas_call x0 -> x1, Pallas kernels: none -> 23.5 us  [stage_body(): pl.pallas_call(weight_grads, grid=(2, 2, GRAD_BLOCKS), out_shape=(jax.Sha...]
    dot_general x2 -> x0, matrix products: 21.6 us -> none  [the longest x1 12 us: stage_body(): grad_first = jnp.einsum('kbd,kbf->kdf', h, e, preferred_element_type=F32)]
where the time goes in v4:
time: 460 us
  Pallas kernels  459 us (100%)
    pallas_call x1, Pallas kernels, stage_body(): pl.pallas_call(functools.partial(pipe_kernel, norm), out_shape=(jax.Shape...  436 us
    pallas_call x1, Pallas kernels, stage_body(): pl.pallas_call(weight_grads, grid=(2, 2, GRAD_BLOCKS), out_shape=(jax.Sha...  23.5 us

profile of v4, /device:TPU:0, one launch (start us, length us, event | category | flops | bytes accessed | tf_op | source)
XLA Modules:
  0.0 459.7 jit_solution(16634426362049326478)
XLA Ops:
  0.6 435.6 %shard_map.67 = (bf16[2,16,32,1536]{3,2,1,0:T(8,128)(2,1)}, bf16[2,16,32,1536]{3,2,1,0:T(8,128)(2,1)}, bf16[2,16,32,1536]{3,2,1,0:T(8,128)(2,1)}, bf16[2,16,32,1536]{3,2,1,0:T(8,128)(2,1)}, f32[8,128]{1,0:T(8,128)}) custom-call(bf16[16,32,1536]{2,1,0:T(8,128)(2,1)} %bitcast.16, bf16[16,32,1536]{2,1,0:T(8,128)(2,1)} %bitcast.17, ...), custom_call_target="tpu_custom_call" | custom-call | tf_op jit(solution)/shard_map/pallas_call | solution.py:383
  436.2 23.5 %shard_map.68 = (f32[2,1536,1536]{2,1,0:T(8,128)}, f32[2,1536,1536]{2,1,0:T(8,128)}, f32[1]{0:T(128)}) custom-call(bf16[2,512,1536]{2,1,0:T(8,128)(2,1)} %bitcast.12, bf16[2,512,1536]{2,1,0:T(8,128)(2,1)} %bitcast.15, bf16[2,512,1536]{2,1,0:T(8,128)(2,1)} %bitcast.14, bf16[2,512,1536]{2,1,0:T(8,128)(2,1)} %bitcast.13, f32[8,128]{1,0:T(8,128)} %get-tuple-element.15.loss_ref), custom_call_target="tpu_custom_call" | custom-call | tf_op jit(solution)/shard_map/pallas_call | solution.py:427

commit v5 on v4

--- a/solution.py
+++ b/solution.py
@@ -356,20 +356,27 @@
         loss_out[...] = loss_dst[...]
 
 
-def weight_grads(h_ref, e_ref, a_ref, g_ref, loss_ref, first_ref, second_ref, total_ref):
-    half = pl.program_id(0)
-
-    def over_tokens(left, right):
-        return lax.dot_general(left, right, (((0,), (0,)), ((), ())), preferred_element_type=F32)
+def weight_grads(h_ref, e_ref, a_ref, g_ref, loss_ref, first_ref, second_ref, total_ref, turned):
+    half, block = pl.program_id(0), pl.program_id(2)
+
+    def over_tokens(left_ref, right_ref, out_ref):
+        rows = out_ref.shape[1]
+
+        @pl.when(block == 0)
+        def _():
+            for i in range(rows // TILE):
+                turned[i * TILE:(i + 1) * TILE, :] = left_ref[0, :, i * TILE:(i + 1) * TILE].T
+
+        out_ref[0] = dot_nn(turned[:rows, :], right_ref[0])
 
     @pl.when(half == 0)
     def _():
         total_ref[0] = jnp.max(loss_ref[...])
-        first_ref[0] = over_tokens(h_ref[0], e_ref[0])
+        over_tokens(h_ref, e_ref, first_ref)
 
     @pl.when(half == 1)
     def _():
-        second_ref[0] = over_tokens(a_ref[0], g_ref[0])
+        over_tokens(a_ref, g_ref, second_ref)
 
 
 def solution(mesh):
@@ -444,6 +451,7 @@
                 pl.BlockSpec((1, hid, width // GRAD_BLOCKS), lambda i, k, j: (k * i, 0, j * i)),
                 pl.BlockSpec(memory_space=pltpu.SMEM),
             ),
+            scratch_shapes=[pltpu.VMEM((max(width, hid), tokens), BF16)],
             compiler_params=pltpu.CompilerParams(vmem_limit_bytes=56 * 1024 * 1024),
         )(h, e, a, g, loss)
         return grad_first[None], grad_second[None], total

time: 460 us -> 462 us (level)
  no operation moved by 1% of the time
where the time goes in v5:
time: 462 us; the launch traced here: 461 us
  Pallas kernels  461 us (100%)
    pallas_call x1, Pallas kernels, stage_body(): pl.pallas_call(functools.partial(pipe_kernel, norm), out_shape=(jax.Shape...  436 us
    pallas_call x1, Pallas kernels, stage_body(): pl.pallas_call(weight_grads, grid=(2, 2, GRAD_BLOCKS), out_shape=(jax.Sha...  25.2 us

profile of v5, /device:TPU:0, one launch (start us, length us, event | category | flops | bytes accessed | tf_op | source)
XLA Modules:
  0.0 461.4 jit_solution(1797793882574637881)
XLA Ops:
  0.6 435.6 %shard_map.67 = (bf16[2,16,32,1536]{3,2,1,0:T(8,128)(2,1)}, bf16[2,16,32,1536]{3,2,1,0:T(8,128)(2,1)}, bf16[2,16,32,1536]{3,2,1,0:T(8,128)(2,1)}, bf16[2,16,32,1536]{3,2,1,0:T(8,128)(2,1)}, f32[8,128]{1,0:T(8,128)}) custom-call(bf16[16,32,1536]{2,1,0:T(8,128)(2,1)} %bitcast.16, bf16[16,32,1536]{2,1,0:T(8,128)(2,1)} %bitcast.17, ...), custom_call_target="tpu_custom_call" | custom-call | tf_op jit(solution)/shard_map/pallas_call | solution.py:390
  436.2 25.2 %shard_map.68 = (f32[2,1536,1536]{2,1,0:T(8,128)}, f32[2,1536,1536]{2,1,0:T(8,128)}, f32[1]{0:T(128)}) custom-call(bf16[2,512,1536]{2,1,0:T(8,128)(2,1)} %bitcast.12, bf16[2,512,1536]{2,1,0:T(8,128)(2,1)} %bitcast.15, bf16[2,512,1536]{2,1,0:T(8,128)(2,1)} %bitcast.14, bf16[2,512,1536]{2,1,0:T(8,128)(2,1)} %bitcast.13, f32[8,128]{1,0:T(8,128)} %get-tuple-element.15.loss_ref), custom_call_target="tpu_custom_call" | custom-call | tf_op jit(solution)/shard_map/pallas_call | solution.py:434

commit v6 on v4

--- a/solution.py
+++ b/solution.py
@@ -356,20 +356,43 @@
         loss_out[...] = loss_dst[...]
 
 
-def weight_grads(h_ref, e_ref, a_ref, g_ref, loss_ref, first_ref, second_ref, total_ref):
-    half = pl.program_id(0)
-
-    def over_tokens(left, right):
-        return lax.dot_general(left, right, (((0,), (0,)), ((), ())), preferred_element_type=F32)
-
-    @pl.when(half == 0)
-    def _():
-        total_ref[0] = jnp.max(loss_ref[...])
-        first_ref[0] = over_tokens(h_ref[0], e_ref[0])
-
-    @pl.when(half == 1)
-    def _():
-        second_ref[0] = over_tokens(a_ref[0], g_ref[0])
+def weight_grads(h_hbm, e_hbm, a_hbm, g_hbm, loss_ref, first_hbm, second_hbm, total_ref, lefts, rights, firsts, seconds, turned, in_sem, out_sem):
+    total_ref[0] = jnp.max(loss_ref[...])
+    jobs = []
+    for k in range(2):
+        jobs.append((0, k, h_hbm, e_hbm, firsts, first_hbm))
+        jobs.append((1, k, a_hbm, g_hbm, seconds, second_hbm))
+
+    def loads(job):
+        kind, k, left, right, _, _ = job
+        rows, columns = left.shape[2], right.shape[2]
+        return (pltpu.make_async_copy(left.at[k], lefts.at[kind, k, :, pl.ds(0, rows)], in_sem.at[kind, k, 0]),
+                pltpu.make_async_copy(right.at[k], rights.at[kind, k, :, pl.ds(0, columns)], in_sem.at[kind, k, 1]))
+
+    def store(job, j):
+        kind, k, _, _, result, out = job
+        width = out.shape[2] // GRAD_BLOCKS
+        return pltpu.make_async_copy(result.at[k, j], out.at[k, :, pl.ds(j * width, width)], out_sem.at[kind, k, j])
+
+    for copy in loads(jobs[0]):
+        copy.start()
+    for number, job in enumerate(jobs):
+        kind, k, left, right, result, out = job
+        rows, width = left.shape[2], right.shape[2] // GRAD_BLOCKS
+        for copy in loads(job):
+            copy.wait()
+        if number == 0:
+            for other in jobs[1:]:
+                for copy in loads(other):
+                    copy.start()
+        for i in range(rows // TILE):
+            turned[i * TILE:(i + 1) * TILE, :] = lefts[kind, k, :, i * TILE:(i + 1) * TILE].T
+        for j in range(GRAD_BLOCKS):
+            result[k, j] = dot_nn(turned[:rows, :], rights[kind, k, :, j * width:(j + 1) * width])
+            store(job, j).start()
+    for job in jobs:
+        for j in range(GRAD_BLOCKS):
+            store(job, j).wait()
 
 
 def solution(mesh):
@@ -426,25 +449,23 @@
         tokens = n * UNIT
         grad_first, grad_second, total = pl.pallas_call(
             weight_grads,
-            grid=(2, 2, GRAD_BLOCKS),
             out_shape=(
                 jax.ShapeDtypeStruct((2, width, hid), F32),
                 jax.ShapeDtypeStruct((2, hid, width), F32),
                 jax.ShapeDtypeStruct((1,), F32),
             ),
-            in_specs=[
-                pl.BlockSpec((1, tokens, width), lambda i, k, j: (k + i * (1 - k), 0, 0)),
-                pl.BlockSpec((1, tokens, hid // GRAD_BLOCKS), lambda i, k, j: (k + i * (1 - k), 0, j + i * (GRAD_BLOCKS - 1 - j))),
-                pl.BlockSpec((1, tokens, hid), lambda i, k, j: (k * i, 0, 0)),
-                pl.BlockSpec((1, tokens, width // GRAD_BLOCKS), lambda i, k, j: (k * i, 0, j * i)),
-                pl.BlockSpec(memory_space=pltpu.VMEM),
+            in_specs=[any_spec] * 4 + [pl.BlockSpec(memory_space=pltpu.VMEM)],
+            out_specs=(any_spec, any_spec, pl.BlockSpec(memory_space=pltpu.SMEM)),
+            scratch_shapes=[
+                pltpu.VMEM((2, 2, tokens, max(width, hid)), BF16),
+                pltpu.VMEM((2, 2, tokens, max(width, hid)), BF16),
+                pltpu.VMEM((2, GRAD_BLOCKS, width, hid // GRAD_BLOCKS), F32),
+                pltpu.VMEM((2, GRAD_BLOCKS, hid, width // GRAD_BLOCKS), F32),
+                pltpu.VMEM((max(width, hid), tokens), BF16),
+                pltpu.SemaphoreType.DMA((2, 2, 2)),
+                pltpu.SemaphoreType.DMA((2, 2, GRAD_BLOCKS)),
             ],
-            out_specs=(
-                pl.BlockSpec((1, width, hid // GRAD_BLOCKS), lambda i, k, j: (k + i * (1 - k), 0, j + i * (GRAD_BLOCKS - 1 - j))),
-                pl.BlockSpec((1, hid, width // GRAD_BLOCKS), lambda i, k, j: (k * i, 0, j * i)),
-                pl.BlockSpec(memory_space=pltpu.SMEM),
-            ),
-            compiler_params=pltpu.CompilerParams(vmem_limit_bytes=56 * 1024 * 1024),
+            compiler_params=pltpu.CompilerParams(vmem_limit_bytes=67043328),
         )(h, e, a, g, loss)
         return grad_first[None], grad_second[None], total
 

time: 460 us -> 454 us (0.987)
  Pallas kernels: 459 us -> 454 us
    pallas_call x1, Pallas kernels: 23.5 us -> 17.9 us  [stage_body(): pl.pallas_call(weight_grads, out_shape=(jax.ShapeDtypeStruct((2, width, h...]
where the time goes in v6:
time: 454 us
  Pallas kernels  454 us (100%)
    pallas_call x1, Pallas kernels, stage_body(): pl.pallas_call(functools.partial(pipe_kernel, norm), out_shape=(jax.Shape...  436 us
    pallas_call x1, Pallas kernels, stage_body(): pl.pallas_call(weight_grads, out_shape=(jax.ShapeDtypeStruct((2, width, h...  17.9 us

profile of v6, /device:TPU:0, one launch (start us, length us, event | category | flops | bytes accessed | tf_op | source)
XLA Modules:
  0.0 454.3 jit_solution(181183855626171108)
XLA Ops:
  0.6 435.6 %shard_map.67 = (bf16[2,16,32,1536]{3,2,1,0:T(8,128)(2,1)}, bf16[2,16,32,1536]{3,2,1,0:T(8,128)(2,1)}, bf16[2,16,32,1536]{3,2,1,0:T(8,128)(2,1)}, bf16[2,16,32,1536]{3,2,1,0:T(8,128)(2,1)}, f32[8,128]{1,0:T(8,128)}) custom-call(bf16[16,32,1536]{2,1,0:T(8,128)(2,1)} %bitcast.16, bf16[16,32,1536]{2,1,0:T(8,128)(2,1)} %bitcast.17, ...), custom_call_target="tpu_custom_call" | custom-call | tf_op jit(solution)/shard_map/pallas_call | solution.py:406
  436.2 17.9 %shard_map.68 = (f32[2,1536,1536]{2,1,0:T(8,128)}, f32[2,1536,1536]{2,1,0:T(8,128)}, f32[1]{0:T(128)}) custom-call(bf16[2,512,1536]{2,1,0:T(8,128)(2,1)} %bitcast.12, bf16[2,512,1536]{2,1,0:T(8,128)(2,1)} %bitcast.15, bf16[2,512,1536]{2,1,0:T(8,128)(2,1)} %bitcast.14, bf16[2,512,1536]{2,1,0:T(8,128)(2,1)} %bitcast.13, f32[8,128]{1,0:T(8,128)} %get-tuple-element.15.loss_ref), custom_call_target="tpu_custom_call" | custom-call | tf_op jit(solution)/shard_map/pallas_call | solution.py:450
